TPU v7x, 128 devices: a whole 4x4x4 slice. The times are simulated.
128 devices in a mesh: trees: 1, data: 128 (over z, y, x, core).
Axes of the slice: x: 4, y: 4, z: 4, core: 2. Of those that a mesh axis runs over, the one named last changes fastest.
Arguments:
- bin_codes: int32 [65536, 3072], P(('trees', 'data'))
- gradient: float32 [65536], P(('trees', 'data'))
- hessian: float32 [65536], P(('trees', 'data'))
- valid_rows: int32 [128], P(('trees', 'data'))
- split_feat: int32 [31], P('trees')
- split_thr: int32 [31], P('trees')
- cut_values: float32 [3072, 15], P('trees')
- reg_lambda: float32 [1], P('trees')
Outputs:
- output 1: float32 [63, 3072, 15], P(None, ('trees', 'data'))
- output 2: float32 [32], P('trees')
- output 3: float32 [31], P('trees')
All inputs are finite; a program needn't handle non-finite values.
Results may differ from a plain program's by a relative error of at most 0.001.
Values sent between devices are 32-bit elements.
A program may use at most 1 GiB of HBM per device.

v0:
```python
import math
import jax
import jax.numpy as jnp
from jax import lax
from jax.sharding import PartitionSpec as P

ONEHOT_CELLS = 4194304


def block_rows(row_count, cell_count):
    blk_rows = row_count
    while blk_rows % 2 == 0 and blk_rows * cell_count > ONEHOT_CELLS:
        blk_rows = blk_rows // 2
    return blk_rows


def local_hist(bin_codes, node_ids, grad_pairs, level_width, bin_count):
    row_count, feat_count = bin_codes.shape
    blk_rows = block_rows(row_count, feat_count * bin_count)
    node_range = jnp.arange(level_width, dtype=jnp.int32)
    weighted = (node_ids[:, None] == node_range[None, :]).astype(jnp.float32)[:, :, None] * grad_pairs[:, None, :]
    bin_ids = jnp.arange(bin_count, dtype=jnp.int32)

    def add_block(blk_index, hist_acc):
        start_row = blk_index * blk_rows
        codes_blk = lax.dynamic_slice_in_dim(bin_codes, start_row, blk_rows, axis=0)
        weight_blk = lax.dynamic_slice_in_dim(weighted, start_row, blk_rows, axis=0)
        onehot = (codes_blk[:, :, None] == bin_ids[None, None, :]).astype(jnp.float32)
        return hist_acc + jnp.einsum('inc,ifb->ncfb', weight_blk, onehot, preferred_element_type=jnp.float32, precision=lax.Precision.HIGHEST)

    hist_zero = jnp.zeros((level_width, 2, feat_count, bin_count), jnp.float32)
    return lax.fori_loop(0, row_count // blk_rows, add_block, hist_zero)


def level_gains(histogram, reg_value):
    last_bin = histogram.shape[3] - 1
    prefix = jnp.cumsum(histogram, axis=3)
    left_sum = prefix[..., :last_bin]
    node_sum = prefix[..., last_bin:]
    right_sum = node_sum - left_sum

    def split_score(pair_sum):
        return pair_sum[:, 0] * pair_sum[:, 0] / (pair_sum[:, 1] + reg_value)

    return 0.5 * (split_score(left_sum) + split_score(right_sum) - split_score(node_sum))


def route(bin_codes, node_ids, split_feat, split_thr, level_width):
    heap_ids = level_width - 1 + node_ids
    feat_row = split_feat[heap_ids]
    thr_row = split_thr[heap_ids]
    feat_ids = jnp.arange(bin_codes.shape[1], dtype=jnp.int32)
    chosen = jnp.sum(jnp.where(feat_ids[None, :] == feat_row[:, None], bin_codes, 0), axis=1)
    return 2 * node_ids + (chosen > thr_row).astype(jnp.int32)


def solution(mesh):
    groups = mesh.shape['data']
    row_spec = P(('trees', 'data'))

    def device_fn(bin_codes, gradient, hessian, valid_rows, split_feat, split_thr, cut_values, reg_lambda):
        row_count, feat_count = bin_codes.shape
        bin_count = cut_values.shape[1] + 1
        depth = int(math.log2(split_feat.shape[0] + 1)) + 1
        feat_local = feat_count // groups
        feat_start = lax.axis_index('data') * feat_local
        reg_value = reg_lambda[0]
        live_rows = jnp.arange(row_count, dtype=jnp.int32) < valid_rows[0]
        grad_pairs = jnp.where(live_rows[:, None], jnp.stack([gradient, hessian], axis=1), 0.0)
        node_ids = jnp.zeros((row_count,), jnp.int32)
        gain_levels = []
        for level in range(depth):
            level_width = 2 ** level
            histogram = lax.psum(local_hist(bin_codes, node_ids, grad_pairs, level_width, bin_count), 'data')
            own_part = lax.dynamic_slice_in_dim(histogram, feat_start, feat_local, axis=2)
            gain_levels.append(level_gains(own_part, reg_value))
            if level < depth - 1:
                node_ids = route(bin_codes, node_ids, split_feat, split_thr, level_width)
        leaf_sum = jnp.sum(histogram[:, :, 0, :], axis=2)
        leaf_value = -leaf_sum[:, 0] / (leaf_sum[:, 1] + reg_value)
        split_value = cut_values[split_feat, split_thr]
        return jnp.concatenate(gain_levels, axis=0), leaf_value, split_value

    return jax.shard_map(device_fn, mesh=mesh, in_specs=(P(('trees', 'data'), None), row_spec, row_spec, row_spec, P('trees'), P('trees'), P('trees', None), P('trees')), out_specs=(P(None, ('trees', 'data'), None), P('trees'), P('trees')), check_vma=False)
```

profile of v0, /device:TPU:1, one launch (start us, length us, event | category | flops | bytes accessed | tf_op | source)
XLA Modules:
  0.0 863.2 jit_solution(17183877738344809748)
XLA Ops:
  19.6 4.2 compare_select_fusion.41
  24.0 4.4 compare_select_fusion.40
  28.3 15.1 %select_select_fusion.3 = s32[512]{0:T(512)S(1)} fusion(pred[512]{0:T(512)(128)(4,1)S(1)} %get-tuple-element.776, pred[512]{0:T(512)(128)(4,1)S(1)} %get-tuple-element.775, pred[512]{0:T(512)(128)(4,1)S(1)} %get-tuple-element.774, pred[512]{0:T(512)(128)(4,1)S(1)} %get-tuple-element.773, pred[512]{0:T(512)(128)(4,1)S(1)} %get-tuple-element.772, ...), kind=kLoop, calls=%fused_computation.335 | loop fusion | flops 12288 | bytes 16480 | tf_op jit(solution)/shard_map/gather | solution.py:50
  44.4 15.1 %broadcast_add_fusion.3 = (s32[512]{0:T(512)S(1)}, s32[512]{0:T(512)S(1)}) fusion(s32[512]{0:T(512)S(1)} %select_reduce_fusion.3, pred[512]{0:T(512)(128)(4,1)S(1)} %get-tuple-element.776, pred[512]{0:T(512)(128)(4,1)S(1)} %get-tuple-element.775, pred[512]{0:T(512)(128)(4,1)S(1)} %get-tuple-element.774, pred[512]{0:T(512)(128)(4,1)S(1)} %get-tuple-element.773, ...), kind=kLoop, calls=%fused_computation.353 | loop fusion | flops 14848 | bytes 21088 | tf_op jit(solution)/shard_map/add | solution.py:49
  59.5 4.2 compare_select_fusion.29
  63.8 4.4 compare_select_fusion.28
  68.3 15.1 %select_select_fusion.2 = s32[512]{0:T(512)S(1)} fusion(pred[512]{0:T(512)(128)(4,1)S(1)} %get-tuple-element.752, pred[512]{0:T(512)(128)(4,1)S(1)} %get-tuple-element.751, pred[512]{0:T(512)(128)(4,1)S(1)} %get-tuple-element.750, pred[512]{0:T(512)(128)(4,1)S(1)} %get-tuple-element.749, pred[512]{0:T(512)(128)(4,1)S(1)} %get-tuple-element.748, ...), kind=kLoop, calls=%fused_computation.333 | loop fusion | flops 12288 | bytes 16480 | tf_op jit(solution)/shard_map/gather | solution.py:50
  84.4 15.1 %broadcast_add_fusion.2 = (s32[512]{0:T(512)S(1)}, s32[512]{0:T(512)S(1)}) fusion(s32[512]{0:T(512)S(1)} %select_reduce_fusion.2, pred[512]{0:T(512)(128)(4,1)S(1)} %get-tuple-element.752, pred[512]{0:T(512)(128)(4,1)S(1)} %get-tuple-element.751, pred[512]{0:T(512)(128)(4,1)S(1)} %get-tuple-element.750, pred[512]{0:T(512)(128)(4,1)S(1)} %get-tuple-element.749, ...), kind=kLoop, calls=%fused_computation.352 | loop fusion | flops 14848 | bytes 22624 | tf_op jit(solution)/shard_map/add | solution.py:49
  99.5 4.2 compare_select_fusion.17
  103.8 4.4 compare_select_fusion.16
  108.3 15.1 %select_select_fusion.1 = s32[512]{0:T(512)S(1)} fusion(pred[512]{0:T(512)(128)(4,1)S(1)} %get-tuple-element.728, pred[512]{0:T(512)(128)(4,1)S(1)} %get-tuple-element.727, pred[512]{0:T(512)(128)(4,1)S(1)} %get-tuple-element.726, pred[512]{0:T(512)(128)(4,1)S(1)} %get-tuple-element.725, pred[512]{0:T(512)(128)(4,1)S(1)} %get-tuple-element.724, ...), kind=kLoop, calls=%fused_computation.331 | loop fusion | flops 12288 | bytes 16480 | tf_op jit(solution)/shard_map/gather | solution.py:50
  124.4 15.1 %broadcast_add_fusion.1 = (s32[512]{0:T(512)S(1)}, s32[512]{0:T(512)S(1)}) fusion(s32[512]{0:T(512)S(1)} %select_reduce_fusion.1, pred[512]{0:T(512)(128)(4,1)S(1)} %get-tuple-element.728, pred[512]{0:T(512)(128)(4,1)S(1)} %get-tuple-element.727, pred[512]{0:T(512)(128)(4,1)S(1)} %get-tuple-element.726, pred[512]{0:T(512)(128)(4,1)S(1)} %get-tuple-element.725, ...), kind=kLoop, calls=%fused_computation.351 | loop fusion | flops 14848 | bytes 22624 | tf_op jit(solution)/shard_map/add | solution.py:49
  143.8 4.4 compare_select_fusion.4
  148.4 15.1 %select_select_fusion = s32[512]{0:T(512)S(1)} fusion(pred[512]{0:T(512)(128)(4,1)S(1)} %get-tuple-element.704, pred[512]{0:T(512)(128)(4,1)S(1)} %get-tuple-element.703, pred[512]{0:T(512)(128)(4,1)S(1)} %get-tuple-element.702, pred[512]{0:T(512)(128)(4,1)S(1)} %get-tuple-element.701, pred[512]{0:T(512)(128)(4,1)S(1)} %get-tuple-element.700, ...), kind=kLoop, calls=%fused_computation.329 | loop fusion | flops 12288 | bytes 16480 | tf_op jit(solution)/shard_map/gather | solution.py:50
  167.2 15.1 %convert_add_fusion = s32[512]{0:T(512)S(1)} fusion(s32[512]{0:T(512)S(1)} %get-tuple-element.834, s32[512]{0:T(512)S(1)} %select_reduce_fusion, pred[512]{0:T(512)(128)(4,1)S(1)} %get-tuple-element.704, pred[512]{0:T(512)(128)(4,1)S(1)} %get-tuple-element.703, pred[512]{0:T(512)(128)(4,1)S(1)} %get-tuple-element.702, ...), kind=kLoop, calls=%fused_computation.336 | loop fusion | flops 14336 | bytes 20576 | tf_op jit(solution)/shard_map/add | solution.py:54
  183.0 107.0 %while.89 = (s32[]{:T(128)}, f32[32,2,3072,16]{2,0,3,1:T(8,128)}, f32[512,32,2]{0,1,2:T(8,128)S(1)}, s32[512,3072]{1,0:T(8,128)}, s32[]{:T(128)}, /*index=5*/s32[]{:T(128)}, s32[]{:T(128)}, s32[]{:T(128)}) while((s32[]{:T(128)}, f32[32,2,3072,16]{2,0,3,1:T(8,128)}, f32[512,32,2]{0,1,2:T(8,128)S(1)}, s32[512,3072]{1,0:T(8,128)}, ...), condition=%wide.region_26.27_spmd.clone, body=%wide.region_25.26_spmd.clone.sunk | while | flops 2425356288 | bytes 27558036 | solution.py:32
  185.3 9.6 %select_add_fusion.5 = f32[32,2,3072,16]{2,0,3,1:T(8,128)} fusion(f32[32,2,3072,16]{2,0,3,1:T(8,128)} %get-tuple-element.1190, s32[64,3072]{1,0:T(8,128)} %constant_dynamic-slice_fusion.23, pred[]{:T(512)S(6)} %compare.903, f32[512,32,2]{0,1,2:T(8,128)S(1)} %get-tuple-element.1199, s32[]{:T(128)S(6)} %select_n.196), kind=kOutput, calls=%fused_computation.53.clone.1 | convolution fusion | flops 2425356288 | bytes 25985028 | tf_op jit(solution)/shard_map/while/body/eval_jaxpr/inc,ifb->ncfb/dot_general | solution.py:29
  196.9 11.5 %select_add_fusion.5 = f32[32,2,3072,16]{2,0,3,1:T(8,128)} fusion(f32[32,2,3072,16]{2,0,3,1:T(8,128)} %get-tuple-element.1190, s32[64,3072]{1,0:T(8,128)} %constant_dynamic-slice_fusion.23, pred[]{:T(512)S(6)} %compare.903, f32[512,32,2]{0,1,2:T(8,128)S(1)} %get-tuple-element.1199, s32[]{:T(128)S(6)} %select_n.196), kind=kOutput, calls=%fused_computation.53.clone.1 | convolution fusion | flops 2425356288 | bytes 25985028 | tf_op jit(solution)/shard_map/while/body/eval_jaxpr/inc,ifb->ncfb/dot_general | solution.py:29
  210.5 11.5 %select_add_fusion.5 = f32[32,2,3072,16]{2,0,3,1:T(8,128)} fusion(f32[32,2,3072,16]{2,0,3,1:T(8,128)} %get-tuple-element.1190, s32[64,3072]{1,0:T(8,128)} %constant_dynamic-slice_fusion.23, pred[]{:T(512)S(6)} %compare.903, f32[512,32,2]{0,1,2:T(8,128)S(1)} %get-tuple-element.1199, s32[]{:T(128)S(6)} %select_n.196), kind=kOutput, calls=%fused_computation.53.clone.1 | convolution fusion | flops 2425356288 | bytes 25985028 | tf_op jit(solution)/shard_map/while/body/eval_jaxpr/inc,ifb->ncfb/dot_general | solution.py:29
  224.1 11.5 %select_add_fusion.5 = f32[32,2,3072,16]{2,0,3,1:T(8,128)} fusion(f32[32,2,3072,16]{2,0,3,1:T(8,128)} %get-tuple-element.1190, s32[64,3072]{1,0:T(8,128)} %constant_dynamic-slice_fusion.23, pred[]{:T(512)S(6)} %compare.903, f32[512,32,2]{0,1,2:T(8,128)S(1)} %get-tuple-element.1199, s32[]{:T(128)S(6)} %select_n.196), kind=kOutput, calls=%fused_computation.53.clone.1 | convolution fusion | flops 2425356288 | bytes 25985028 | tf_op jit(solution)/shard_map/while/body/eval_jaxpr/inc,ifb->ncfb/dot_general | solution.py:29
  237.7 11.5 %select_add_fusion.5 = f32[32,2,3072,16]{2,0,3,1:T(8,128)} fusion(f32[32,2,3072,16]{2,0,3,1:T(8,128)} %get-tuple-element.1190, s32[64,3072]{1,0:T(8,128)} %constant_dynamic-slice_fusion.23, pred[]{:T(512)S(6)} %compare.903, f32[512,32,2]{0,1,2:T(8,128)S(1)} %get-tuple-element.1199, s32[]{:T(128)S(6)} %select_n.196), kind=kOutput, calls=%fused_computation.53.clone.1 | convolution fusion | flops 2425356288 | bytes 25985028 | tf_op jit(solution)/shard_map/while/body/eval_jaxpr/inc,ifb->ncfb/dot_general | solution.py:29
  251.2 11.5 %select_add_fusion.5 = f32[32,2,3072,16]{2,0,3,1:T(8,128)} fusion(f32[32,2,3072,16]{2,0,3,1:T(8,128)} %get-tuple-element.1190, s32[64,3072]{1,0:T(8,128)} %constant_dynamic-slice_fusion.23, pred[]{:T(512)S(6)} %compare.903, f32[512,32,2]{0,1,2:T(8,128)S(1)} %get-tuple-element.1199, s32[]{:T(128)S(6)} %select_n.196), kind=kOutput, calls=%fused_computation.53.clone.1 | convolution fusion | flops 2425356288 | bytes 25985028 | tf_op jit(solution)/shard_map/while/body/eval_jaxpr/inc,ifb->ncfb/dot_general | solution.py:29
  264.8 11.5 %select_add_fusion.5 = f32[32,2,3072,16]{2,0,3,1:T(8,128)} fusion(f32[32,2,3072,16]{2,0,3,1:T(8,128)} %get-tuple-element.1190, s32[64,3072]{1,0:T(8,128)} %constant_dynamic-slice_fusion.23, pred[]{:T(512)S(6)} %compare.903, f32[512,32,2]{0,1,2:T(8,128)S(1)} %get-tuple-element.1199, s32[]{:T(128)S(6)} %select_n.196), kind=kOutput, calls=%fused_computation.53.clone.1 | convolution fusion | flops 2425356288 | bytes 25985028 | tf_op jit(solution)/shard_map/while/body/eval_jaxpr/inc,ifb->ncfb/dot_general | solution.py:29
  278.4 11.5 %select_add_fusion.5 = f32[32,2,3072,16]{2,0,3,1:T(8,128)} fusion(f32[32,2,3072,16]{2,0,3,1:T(8,128)} %get-tuple-element.1190, s32[64,3072]{1,0:T(8,128)} %constant_dynamic-slice_fusion.23, pred[]{:T(512)S(6)} %compare.903, f32[512,32,2]{0,1,2:T(8,128)S(1)} %get-tuple-element.1199, s32[]{:T(128)S(6)} %select_n.196), kind=kOutput, calls=%fused_computation.53.clone.1 | convolution fusion | flops 2425356288 | bytes 25985028 | tf_op jit(solution)/shard_map/while/body/eval_jaxpr/inc,ifb->ncfb/dot_general | solution.py:29
  290.0 77.8 %while.88 = (s32[]{:T(128)}, f32[16,2,3072,16]{2,0,3,1:T(8,128)}, f32[512,16,2]{0,1,2:T(8,128)S(1)}, s32[512,3072]{1,0:T(8,128)}, s32[]{:T(128)}, /*index=5*/s32[]{:T(128)}, s32[]{:T(128)}, s32[]{:T(128)}) while((s32[]{:T(128)}, f32[16,2,3072,16]{2,0,3,1:T(8,128)}, f32[512,16,2]{0,1,2:T(8,128)S(1)}, s32[512,3072]{1,0:T(8,128)}, ...), condition=%wide.region_21.22_spmd.clone, body=%wide.region_20.21_spmd.clone.sunk | while | flops 1214251008 | bytes 14958741 | solution.py:32
  292.0 6.8 select_add_fusion.4
  300.9 7.8 select_add_fusion.4
  310.7 7.8 select_add_fusion.4
  320.6 7.8 select_add_fusion.4
  330.4 7.8 select_add_fusion.4
  340.2 7.8 select_add_fusion.4
  350.1 7.8 select_add_fusion.4
  359.9 7.8 select_add_fusion.4
  367.7 54.7 %while.87 = (s32[]{:T(128)}, f32[8,2,3072,16]{2,0,3,1:T(8,128)S(1)}, f32[512,8,2]{0,1,2:T(8,128)S(1)}, s32[512,3072]{1,0:T(8,128)}, s32[]{:T(128)}, /*index=5*/s32[]{:T(128)}, s32[]{:T(128)}, s32[]{:T(128)}) while((s32[]{:T(128)}, f32[8,2,3072,16]{2,0,3,1:T(8,128)S(1)}, f32[512,8,2]{0,1,2:T(8,128)S(1)}, s32[512,3072]{1,0:T(8,128)}, ...), condition=%wide.region_16.17_spmd.clone, body=%wide.region_15.16_spmd.clone.sunk | while | flops 608698368 | bytes 8659093 | solution.py:32
  369.8 4.7 fusion.153
  376.7 4.7 fusion.153
  383.5 4.7 fusion.153
  390.3 4.8 fusion.153
  397.2 4.7 fusion.153
  404.0 4.7 fusion.153
  410.8 4.7 fusion.153
  417.7 4.7 fusion.153
  424.1 64.0 %while.86 = (s32[]{:T(128)}, f32[4,2,3072,16]{2,0,3,1:T(4,128)}, f32[512,4,2]{0,1,2:T(4,128)S(1)}, s32[512,3072]{1,0:T(8,128)}, s32[]{:T(128)}, /*index=5*/s32[]{:T(128)}, s32[]{:T(128)}, s32[]{:T(128)}) while((s32[]{:T(128)}, f32[4,2,3072,16]{2,0,3,1:T(4,128)}, f32[512,4,2]{0,1,2:T(4,128)S(1)}, s32[512,3072]{1,0:T(8,128)}, ...), condition=%wide.region_11.12_spmd.clone, body=%wide.region_10.11_spmd.clone.sunk | while | flops 305922048 | bytes 5509269 | solution.py:32
  426.1 5.7 fusion.150
  433.9 6.0 fusion.150
  441.9 6.0 fusion.150
  450.0 6.0 fusion.150
  458.0 6.0 fusion.150
  466.0 6.0 fusion.150
  474.1 6.0 fusion.150
  482.1 6.0 fusion.150
  488.1 53.6 %while.85 = (s32[]{:T(128)}, f32[2,2,3072,16]{2,1,3,0:T(2,128)}, f32[512,2,2]{0,2,1:T(2,128)S(1)}, s32[512,3072]{1,0:T(8,128)}, s32[]{:T(128)}, /*index=5*/s32[]{:T(128)}, s32[]{:T(128)}, s32[]{:T(128)}) while((s32[]{:T(128)}, f32[2,2,3072,16]{2,1,3,0:T(2,128)}, f32[512,2,2]{0,2,1:T(2,128)S(1)}, s32[512,3072]{1,0:T(8,128)}, ...), condition=%wide.region_6.7_spmd.clone, body=%wide.region_5.6_spmd.clone.sunk | while | flops 154533888 | bytes 3934357 | solution.py:32
  489.5 4.6 fusion.147
  495.4 5.6 fusion.147
  502.2 5.6 fusion.147
  509.0 5.6 fusion.147
  515.8 5.6 fusion.147
  522.5 5.6 fusion.147
  529.3 5.6 fusion.147
  536.1 5.6 fusion.147
  541.7 40.5 %while.84 = (s32[]{:T(128)}, f32[1,2,3072,16]{2,1,3,0:T(2,128)S(1)}, f32[512,1,2]{0,2,1:T(2,128)S(1)}, s32[512,3072]{1,0:T(8,128)}, s32[]{:T(128)}, /*index=5*/s32[]{:T(128)}, s32[]{:T(128)}, s32[]{:T(128)}) while((s32[]{:T(128)}, f32[1,2,3072,16]{2,1,3,0:T(2,128)S(1)}, f32[512,1,2]{0,2,1:T(2,128)S(1)}, s32[512,3072]{1,0:T(8,128)}, ...), condition=%wide.region_1.2_spmd.clone, body=%wide.region_0.1_spmd.clone.sunk | while | flops 78839816 | bytes 3146901 | solution.py:32
  585.0 232.6 %all-reduce.3.cloned.1.call-done = (f32[1,2,3072,16]{2,1,3,0:T(2,128)}, f32[2,2,3072,16]{2,1,3,0:T(2,128)}, f32[4,2,3072,16]{2,0,3,1:T(4,128)}, f32[8,2,3072,16]...) async-done(((f32[1,2,3072,16]{2,1,3,0:T(2,128)}, f32[2,2,3072,16]{2,1,3,0:T(2,128)}, f32[4,2,3072,16]{2,0,3,1:T(4,128)}, ...) | async-done | bytes 24772624 | tf_op jit(solution)/shard_map/psum | solution.py:74
  819.4 11.0 %reduce_window_sum.71 = f32[32,2,24,16]{3,2,1,0:T(8,128)S(1)} reduce-window(f32[32,2,24,16]{3,2,1,0:T(8,128)S(1)} %copy.62, f32[]{:T(128)} %constant.222.clone.1), window={size=1x1x1x16 pad=0_0x0_0x0_0x15_0}, to_apply=%region_28.29 | reduce-window | flops 368640 | bytes 196612 | tf_op jit(solution)/shard_map/jit(cumsum)/reduce_window_sum | solution.py:37
  835.2 5.5 reduce_window_sum.70
  (176 shorter events, 165.4 us)
Async XLA Ops:
  7.2 576.5 %copy-start = (f32[3072,15]{0,1:T(8,128)S(1)}, f32[3072,15]{0,1:T(8,128)}, u32[]{:S(2)}) copy-start(f32[3072,15]{0,1:T(8,128)} %param.26) | copy-start | bytes 552964
  7.2 810.4 %all-reduce.3.cloned.1.call-start = ((), (), s32[]{:S(2)}) async-start(), calls=%async_computation | async-start | bytes 49545216 | tf_op jit(solution)/shard_map/psum | solution.py:74
  7.2 36.2 %copy-start.1 = (s32[512,3072]{1,0:T(8,128)S(1)}, s32[512,3072]{1,0:T(8,128)}, u32[]{:S(2)}) copy-start(s32[512,3072]{1,0:T(8,128)} %param.20) | copy-start | bytes 18874372
  123.3 59.6 %copy-start.7 = (f32[512]{0:T(512)S(1)}, f32[512]{0:T(512)}, u32[]{:S(2)}) copy-start(f32[512]{0:T(512)} %param.22) | copy-start | bytes 6148
  123.4 59.6 %copy-start.8 = (f32[512]{0:T(512)S(1)}, f32[512]{0:T(512)}, u32[]{:S(2)}) copy-start(f32[512]{0:T(512)} %param.21) | copy-start | bytes 6148
  422.4 1.6 copy-start.2
  488.1 53.6 %copy-start.5 = (f32[1,2,3072,16]{2,1,3,0:T(2,128)S(1)}, f32[1,2,3072,16]{2,1,3,0:T(2,128)}, u32[]{:S(2)}) copy-start(f32[1,2,3072,16]{2,1,3,0:T(2,128)} %custom-call.2) | copy-start | bytes 1179652
  582.2 0.7 copy-start.6
  582.2 1.4 copy-start.3
  582.2 1.4 copy-start.4
Sparse Core Ops, SparseCore 0:
  583.1 234.4 all-reduce.2
where the time goes:
time: 869 us; the launch traced here: 863 us
  matrix products  312 us (36%)
  waiting for transfers between devices  233 us (27%)
  other arithmetic  193 us (22%)
  local copies, waits for them, and re-layouts  109 us (13%)
  between operations  16 us (2%)
    dot_general x48, matrix products, add_block(): jnp.einsum('inc,ifb->ncfb', weight_blk, onehot, preferred_element_type=jn...  312 us
    psum x1, waiting for transfers between devices, device_fn(): lax.psum(local_hist(bin_codes, node_ids, grad_pairs, level_width, bin_cou...  233 us
    dynamic_slice x48, local copies, waits for them, and re-layouts, add_block(): codes_blk = lax.dynamic_slice_in_dim(bin_codes, start_row, blk_rows, axis=0)  84.8 us
    gather x12, other arithmetic, route(): feat_row = split_feat[heap_ids]  78.3 us
    add x4, other arithmetic, route(): heap_ids = level_width - 1 + node_ids  45.8 us
    another operation x6, other arithmetic, level_gains(): prefix = jnp.cumsum(histogram, axis=3)  21.6 us
  transfers between devices with their start and end apart: 1, of which 1 were waited for; matrix products, arithmetic and copies ran while one was open for 0% of the time, Pallas kernels for 0%

commit v1 on v0

v1 whole, which is shorter than its diff:
```python
import math
import jax
import jax.numpy as jnp
from jax import lax
from jax.sharding import PartitionSpec as P


def route(codes, split_feat, split_thr, depth):
    columns = codes[:, split_feat]
    goes_right = columns > split_thr[None, :]
    node = jnp.zeros((codes.shape[0],), jnp.int32)
    inner = jnp.arange(split_feat.shape[0], dtype=jnp.int32)
    heap = node
    for _ in range(depth - 1):
        bit = jnp.any((heap[:, None] == inner[None, :]) & goes_right, axis=1)
        heap = 2 * heap + 1 + bit.astype(jnp.int32)
    return heap - (2 ** (depth - 1) - 1)


def solution(mesh):
    groups = mesh.shape['data']
    row_spec = P(('trees', 'data'))

    def device_fn(bin_codes, gradient, hessian, valid_rows, split_feat, split_thr, cut_values, reg_lambda):
        row_count, feat_count = bin_codes.shape
        bin_count = cut_values.shape[1] + 1
        depth = int(math.log2(split_feat.shape[0] + 1)) + 1
        leaves = 2 ** (depth - 1)
        reg_value = reg_lambda[0]
        live_rows = jnp.arange(row_count, dtype=jnp.int32) < valid_rows[0]
        leaf = route(bin_codes, split_feat, split_thr, depth)
        pairs = jnp.where(live_rows[:, None], jnp.stack([gradient, hessian], axis=1), 0.0)
        in_leaf = leaf[:, None] == jnp.arange(leaves, dtype=jnp.int32)[None, :]
        weighted = jnp.where(in_leaf[:, None, :], pairs[:, :, None], 0.0).reshape(row_count, 2 * leaves)
        bins = jnp.arange(bin_count, dtype=jnp.int32)
        below = (bin_codes[:, None, :] <= bins[None, :, None]).astype(jnp.float32)
        part = jnp.einsum('im,ibf->fbm', weighted, below, preferred_element_type=jnp.float32, precision=lax.Precision.HIGHEST)
        own = lax.psum_scatter(part, 'data', scatter_dimension=0, tiled=True)
        own = own.reshape(own.shape[0], bin_count, 2, leaves)
        levels = [own]
        for _ in range(depth - 1):
            last = levels[0]
            levels.insert(0, last.reshape(last.shape[:-1] + (last.shape[-1] // 2, 2)).sum(-1))
        sums = jnp.concatenate(levels, axis=-1)
        left = sums[:, :bin_count - 1]
        total = sums[:, bin_count - 1:]
        right = total - left

        def score(v):
            return v[:, :, 0] * v[:, :, 0] / (v[:, :, 1] + reg_value)

        gain = 0.5 * (score(left) + score(right) - score(total))
        leaf_sum = own[0, bin_count - 1]
        leaf_value = -leaf_sum[0] / (leaf_sum[1] + reg_value)
        split_value = cut_values[split_feat, split_thr]
        return jnp.transpose(gain, (2, 0, 1)), leaf_value, split_value

    return jax.shard_map(device_fn, mesh=mesh, in_specs=(P(('trees', 'data'), None), row_spec, row_spec, row_spec, P('trees'), P('trees'), P('trees', None), P('trees')), out_specs=(P(None, ('trees', 'data'), None), P('trees'), P('trees')), check_vma=False)
```

time: 869 us -> 342 us (0.39)
  matrix products: 312 us -> 37.8 us
  other arithmetic: 193 us -> 2.45 us
  local copies, waits for them, and re-layouts: 109 us -> 37.1 us
  waiting for transfers between devices: 233 us -> 247 us
    dot_general x48 -> x1, matrix products: 312 us -> 37.8 us  [device_fn(): jnp.einsum('im,ibf->fbm', weighted, below, preferred_element_type=jnp.flo...]
    reduce_scatter x0 -> x1, waiting for transfers between devices: none -> 247 us  [device_fn(): own = lax.psum_scatter(part, 'data', scatter_dimension=0, tiled=True)]
    psum x1 -> x0, waiting for transfers between devices: 233 us -> none  [device_fn(): lax.psum(local_hist(bin_codes, node_ids, grad_pairs, level_width, bin_cou...]
    gather x16 -> x1, other arithmetic: 95.2 us -> 0.01 us  [route(): columns = codes[:, split_feat]]
    dynamic_slice x60 -> x0, local copies, waits for them, and re-layouts: 92.2 us -> none  [the longest x48 84.8 us: add_block(): codes_blk = lax.dynamic_slice_in_dim(bin_codes, start_row, blk_rows, axis=0)]
    add x9 -> x3, other arithmetic: 60.9 us -> 0.04 us  [route(): heap = 2 * heap + 1 + bit.astype(jnp.int32)]
    another operation x6 -> x1, other arithmetic: 21.6 us -> 0.01 us  [route(): heap = 2 * heap + 1 + bit.astype(jnp.int32)]
    transpose x0 -> x1, local copies, waits for them, and re-layouts: none -> 21 us  [device_fn(): jnp.einsum('im,ibf->fbm', weighted, below, preferred_element_type=jnp.flo...]
where the time goes in v1:
time: 342 us; the launch traced here: 340 us
  waiting for transfers between devices  247 us (72%)
  matrix products  37.8 us (11%)
  local copies, waits for them, and re-layouts  37.1 us (11%)
  between operations  15.5 us (5%)
    reduce_scatter x1, waiting for transfers between devices, device_fn(): own = lax.psum_scatter(part, 'data', scatter_dimension=0, tiled=True)  247 us
    dot_general x1, matrix products, device_fn(): jnp.einsum('im,ibf->fbm', weighted, below, preferred_element_type=jnp.flo...  37.8 us
    transpose x1, local copies, waits for them, and re-layouts, device_fn(): jnp.einsum('im,ibf->fbm', weighted, below, preferred_element_type=jnp.flo...  21 us
  transfers between devices with their start and end apart: 1, of which 1 were waited for; matrix products, arithmetic and copies ran while one was open for 0% of the time, Pallas kernels for 0%

profile of v1, /device:TPU:1, one launch (start us, length us, event | category | flops | bytes accessed | tf_op | source)
XLA Modules:
  0.0 339.5 jit_solution(2862003935505706620)
XLA Ops:
  7.2 0.0 copy-start
  7.2 0.0 copy-start.1
  7.2 0.0 copy-start.3
  7.2 0.0 copy-start.2
  7.2 0.0 reduce-scatter.2.cloned.1.call-start
  7.3 0.7 fusion.23
  8.0 6.6 %copy.35 = s32[512,3072]{0,1:T(8,128)} copy(s32[512,3072]{1,0:T(8,128)} %param.8) | data formatting | bytes 12582912 | tf_op args[0]
  14.6 3.4 %gather_fusion = s32[31,512]{1,0:T(8,128)S(1)} fusion(s32[512,3072]{0,1:T(8,128)} %copy.35, s32[1024]{0:T(1024)S(1)} %pad_clamp_fusion), kind=kCustom, calls=%fused_computation | custom fusion | bytes 127100 | tf_op jit(solution)/shard_map/gather | solution.py:9
  18.0 0.0 copy-done.1
  18.0 0.1 fusion.18
  19.0 0.0 copy-done.3
  19.0 0.0 copy-done.2
  19.0 37.8 %fusion.2 = f32[3072,16,64]{0,2,1:T(8,128)} fusion(f32[512,64,1]{0,1,2:T(8,128)S(1)} %bitcast.50, s32[512,3072]{1,0:T(8,128)} %param.8), kind=kOutput, calls=%fused_computation.5 | convolution fusion | flops 19352518656 | bytes 19005440 | tf_op jit(solution)/shard_map/im,ibf->fbm/dot_general | solution.py:37
  56.8 21.0 %copy.36 = f32[3072,16,64]{2,1,0:T(8,128)} copy(f32[3072,16,64]{0,2,1:T(8,128)} %fusion.2) | data formatting | bytes 25165824 | tf_op jit(solution)/shard_map/im,ibf->fbm/transpose | solution.py:37
  77.8 0.0 reduce-scatter.2.cloned.1.call-update
  78.5 0.0 copy-done
  78.5 1.3 gather_fusion.1
  79.8 246.7 %reduce-scatter.2.cloned.1.call-done = f32[24,16,64]{2,1,0:T(8,128)} async-done(((f32[3072,16,64]{2,1,0:T(8,128)}), f32[24,16,64]{2,1,0:T(8,128)}) %reduce-scatter.2.cloned.1.call-update) | async-done | bytes 98320 | tf_op jit(solution)/shard_map/reduce_scatter | solution.py:38
  326.5 1.2 copy.37
  327.7 0.1 bitcast_reduce_fusion.1
  327.8 0.2 copy.46
  328.0 0.2 copy.45
  328.2 0.3 copy.44
  328.5 0.3 copy.43
  328.8 0.3 copy.42
  329.0 1.2 reshape.168
  330.2 0.2 copy.47
  330.4 0.9 concatenate.10
  331.4 0.5 fusion.25
  331.9 0.7 fusion.8
  (22 shorter events, 0.4 us)
Async XLA Ops:
  7.2 71.3 %copy-start = (f32[3072,15]{0,1:T(8,128)S(1)}, f32[3072,15]{0,1:T(8,128)}, u32[]{:S(2)}) copy-start(f32[3072,15]{0,1:T(8,128)} %param.14) | copy-start | bytes 552964
  7.2 10.8 %copy-start.1 = (s32[31]{0:T(128)S(1)}, s32[31]{0:T(128)}, u32[]{:S(2)}) copy-start(s32[31]{0:T(128)} %param.13) | copy-start | bytes 376
  7.2 11.8 %copy-start.3 = (f32[512]{0:T(512)S(1)}, f32[512]{0:T(512)}, u32[]{:S(2)}) copy-start(f32[512]{0:T(512)} %param.9) | copy-start | bytes 6148
  7.2 11.8 %copy-start.2 = (f32[512]{0:T(512)S(1)}, f32[512]{0:T(512)}, u32[]{:S(2)}) copy-start(f32[512]{0:T(512)} %param.10) | copy-start | bytes 6148
  7.2 319.2 %reduce-scatter.2.cloned.1.call-start = ((), (), s32[]{:S(2)}) async-start(), calls=%async_computation.1 | async-start | bytes 25362432 | tf_op jit(solution)/shard_map/reduce_scatter | solution.py:38
Sparse Core Ops, SparseCore 0:
  77.9 248.4 reduce-scatter.1

commit v2 on v1

v2 whole, which is shorter than its diff:
```python
import functools
import jax
import jax.numpy as jnp
from jax import lax
from jax.experimental import pallas as pl
from jax.experimental.pallas import tpu as pltpu
from jax.sharding import PartitionSpec as P

F32 = jnp.float32
BF16 = jnp.bfloat16
ROWS = 512
FEATS = 3072
BINS = 16
LEAVES = 32
INNER = 31
LOADS = 8
SLAB = FEATS // LOADS


def pow4(dim):
    return 1 + 3 * dim * (3 * dim - 1) // 2


def coord(me, dim):
    return (me // 2) // pow4(dim) % 4


def neighbour(me, dim, step):
    at = coord(me, dim)
    return me + ((at + step + 4) % 4 - at) * 2 * pow4(dim)


def hist_kernel(codes_hbm, grad_ref, hess_ref, valid_ref, feat_ref, thr_ref, out_ref,
                raw, turned, turned_rx, codes2, meta, weights, hist, rx1, rx2, rx3,
                load_sem, pair_send, pair_recv, send_sem, recv_sem):
    me = lax.axis_index('data')
    core = me % 2
    partner = me + 1 - 2 * core

    def remote(src, dst, s_sem, r_sem, device):
        return pltpu.make_async_remote_copy(src_ref=src, dst_ref=dst, send_sem=s_sem, recv_sem=r_sem, device_id=(0, device), device_id_type=pl.DeviceIdType.MESH)

    barrier = pltpu.get_barrier_semaphore()
    pl.semaphore_signal(barrier, inc=1, device_id=(0, partner), device_id_type=pl.DeviceIdType.MESH)
    for dim in range(3):
        for step in (1, -1):
            pl.semaphore_signal(barrier, inc=1, device_id=(0, neighbour(me, dim, step)), device_id_type=pl.DeviceIdType.MESH)

    def load(m):
        return pltpu.make_async_copy(codes_hbm.at[:, pl.ds(m * SLAB, SLAB)], raw.at[m], load_sem.at[m])

    for m in range(LOADS):
        load(m).start()
    pl.semaphore_wait(barrier, 7)

    def pair_copy(m):
        return remote(turned.at[pl.ds(m * 8, 8), 1 - core], turned_rx.at[pl.ds(m * 8, 8)], pair_send.at[m], pair_recv.at[m], partner)

    meta_copy = remote(meta.at[0], meta.at[1], pair_send.at[LOADS], pair_recv.at[LOADS], partner)

    @pl.loop(0, LOADS)
    def _(m):
        pltpu.make_async_copy(codes_hbm.at[:, pl.ds(0, SLAB)], raw.at[m], load_sem.at[m]).wait()
        block = raw[m].astype(F32)
        turned[pl.ds(m * 8, 8)] = block.T.reshape(8, 2, 24, ROWS)
        pair_copy(m).start()

    def goes_right(j):
        feat = feat_ref[j]
        column = turned[feat // 48, feat // 24 % 2, pl.ds(feat % 24, 1), :]
        return (column > thr_ref[j].astype(F32)).astype(jnp.int32)

    leaf = goes_right(0)
    for level in range(1, 5):
        width = 2 ** level
        bit = goes_right(width - 1)
        for n in range(1, width):
            bit = jnp.where(leaf == n, goes_right(width - 1 + n), bit)
        leaf = 2 * leaf + bit
    live = lax.broadcasted_iota(jnp.int32, (1, ROWS), 1) < valid_ref[0]
    grad = jnp.where(live, grad_ref[...], 0.0)
    hess = jnp.where(live, hess_ref[...], 0.0)
    meta[0] = jnp.concatenate([grad, hess, leaf.astype(F32), jnp.zeros((5, ROWS), F32)], axis=0)
    meta_copy.start()

    def split3(v):
        hi = v.astype(BF16).astype(F32)
        mid = (v - hi).astype(BF16).astype(F32)
        return hi, mid, v - hi - mid

    def fill_weights(side):
        for k in range(ROWS // 128):
            lanes = pl.ds(k * 128, 128)
            g3 = split3(meta[side, 0:1, lanes])
            h3 = split3(meta[side, 1:2, lanes])
            hit = meta[side, 2:3, lanes] == lax.broadcasted_iota(jnp.int32, (LEAVES, 128), 0).astype(F32)
            rows = []
            for i in range(3):
                rows.append(jnp.where(hit, g3[i], 0.0))
                rows.append(jnp.where(hit, h3[i], 0.0))
            rows.append(jnp.zeros((64, 128), F32))
            weights[pl.ds(side * ROWS + k * 128, 128), :] = jnp.concatenate(rows, axis=0).T.astype(BF16)

    fill_weights(0)

    def fill_codes(source, lane0, chip):
        where = (chip % 4, chip // 4 % 4, chip // 16)
        for p in range(3):
            v = source(p)
            codes2[p, where[p], where[(p + 1) % 3], where[(p + 2) % 3], :, pl.ds(lane0, ROWS)] = jnp.concatenate([v, v - 1.0], axis=0).astype(BF16)

    @pl.loop(0, 64, unroll=4)
    def _(chip):
        fill_codes(lambda p: turned[chip, core, pl.ds(8 * p, 8), :], 0, chip)

    meta_copy.wait_recv()
    fill_weights(1)

    @pl.loop(0, LOADS)
    def _(m):
        pair_copy(m).wait_recv()
        for k in range(8):
            chip = m * 8 + k
            fill_codes(lambda p: turned_rx[chip, pl.ds(8 * p, 8), :], ROWS, chip)

    def block(ph, c, p, half, j):
        if ph == 0:
            return hist.at[p, c, j, half]
        ia = coord(me, p)
        if ph == 1:
            return hist.at[p, c, ia, half, j]
        return hist.at[p, c, ia, half, coord(me, (p + 1) % 3), pl.ds(2 * j, 2)]

    def landing(ph, c, p, kind, half):
        return (rx1, rx2, rx3)[ph].at[p, c, kind, half]

    def copy(ph, c, p, kind, half):
        dim = (p + ph) % 3
        at = coord(me, dim)
        step = 1 if (kind == 1) == (half == 1) else -1
        j = (at + 2) % 4 if kind == 0 else (at + step + 4) % 4
        s = ((ph * 2 + c) * 3 + p) * 6 + kind * 2 + half
        return remote(block(ph, c, p, half, j), landing(ph, c, p, kind, half), send_sem.at[s], recv_sem.at[s], neighbour(me, dim, step))

    def send_far(ph, c, p):
        copy(ph, c, p, 0, 0).start()
        copy(ph, c, p, 0, 1).start()

    def send_near(ph, c, p):
        copy(ph, c, p, 1, 1).start()
        copy(ph, c, p, 1, 0).start()

    def relay(ph, c, p):
        at = coord(me, (p + ph) % 3)
        for half in range(2):
            copy(ph, c, p, 0, half).wait_recv()
            mine = block(ph, c, p, half, (at + (1, 3)[half]) % 4)
            mine[...] = mine[...] + landing(ph, c, p, 0, half)[...]
            copy(ph, c, p, 2, half).start()

    def collect(ph, c, p):
        at = coord(me, (p + ph) % 3)
        for half in range(2):
            copy(ph, c, p, 1, half).wait_recv()
            copy(ph, c, p, 2, half).wait_recv()
            mine = block(ph, c, p, half, at)
            mine[...] = mine[...] + landing(ph, c, p, 1, half)[...] + landing(ph, c, p, 2, half)[...]

    def collect_and_send(ph, c, p):
        collect(ph, c, p)
        send_far(ph + 1, c, p)
        send_near(ph + 1, c, p)

    first_half = lax.broadcasted_iota(jnp.int32, (64, 8, 128), 2) < 64

    def unit(c, p, ja):
        pieces = []
        for half in range(2):
            for jb in range(4):
                for jc in range(4):
                    code = codes2[p, ja, jb, jc]
                    for q in range(2):
                        bound = 2.0 * (c * 4 + half * 2 + q)
                        pieces.append(jnp.where(code <= jnp.asarray(bound, BF16), jnp.asarray(1, BF16), jnp.asarray(0, BF16)))
        left = jnp.concatenate(pieces, axis=0)
        sums = jnp.dot(left, weights[...], preferred_element_type=F32)
        sums = (sums[:, :128] + sums[:, 128:]).reshape(64, 2, 8, 128)
        even, odd = sums[:, 0], sums[:, 1]
        keep = jnp.where(first_half, even, odd)
        turn = jnp.where(first_half, odd, even).reshape(512, 128)
        both = keep + pltpu.roll(turn, 64, 1).reshape(64, 8, 128)
        hist[p, c, ja] = both.reshape(2, 4, 8, 8, 128)

    for c in range(2):
        @pl.loop(0, 12)
        def _(u):
            p, jj = u % 3, u // 3
            ahead = (2 + 3 * jj + (jj // 2) * (7 - 2 * jj)) % 4
            unit(c, p, (coord(me, p) + ahead) % 4)

            @pl.when(jj == 0)
            def _():
                send_far(0, c, p)

            @pl.when(jj == 1)
            def _():
                copy(0, c, p, 1, 1).start()

            @pl.when(jj == 2)
            def _():
                copy(0, c, p, 1, 0).start()
                if c == 1:
                    collect_and_send(0, 0, p)

            @pl.when(jj == 3)
            def _():
                if c == 1:
                    relay(1, 0, p)
                relay(0, c, p)

    def for_parts(task):
        @pl.loop(0, 3)
        def _(p):
            task(p)

    for_parts(lambda p: collect_and_send(1, 0, p))
    for_parts(lambda p: collect_and_send(0, 1, p))
    for_parts(lambda p: relay(2, 0, p))
    for_parts(lambda p: relay(1, 1, p))
    for_parts(lambda p: collect(2, 0, p))
    for_parts(lambda p: collect_and_send(1, 1, p))
    for_parts(lambda p: relay(2, 1, p))
    for_parts(lambda p: collect(2, 1, p))

    def deliver(p):
        for c in range(2):
            for half in range(2):
                out_ref[p, c, half] = block(2, c, p, half, coord(me, (p + 2) % 3))[...]

    for_parts(deliver)

    meta_copy.wait_send()

    @pl.loop(0, LOADS)
    def _(m):
        pair_copy(m).wait_send()

    for ph in range(3):
        for c in range(2):
            @pl.loop(0, 3)
            def _(p):
                for kind in range(3):
                    for half in range(2):
                        copy(ph, c, p, kind, half).wait_send()


def gain_kernel(sums_ref, cut_ref, feat_ref, thr_ref, reg_ref, gain_ref, leaf_ref, value_ref):
    reg = reg_ref[0]
    sums = sums_ref[...].reshape(192, 128)
    lane = lax.broadcasted_iota(jnp.int32, (128, 256), 0)
    col = lax.broadcasted_iota(jnp.int32, (128, 256), 1)
    same = (lane // 64 == col // 64 % 2) & (lane // 32 % 2 == col // 128)
    under = lane % 32 + 32
    hit = under == col % 64 + 1
    for _ in range(5):
        under = under // 2
        hit = hit | (under == col % 64 + 1)
    pick = jnp.where(same & hit, 1.0, 0.0).astype(BF16)
    hi = sums.astype(BF16)
    rest = sums - hi.astype(F32)
    mid = rest.astype(BF16)
    low = (rest - mid.astype(F32)).astype(BF16)
    nodes = jnp.dot(low, pick, preferred_element_type=F32) + jnp.dot(mid, pick, preferred_element_type=F32) + jnp.dot(hi, pick, preferred_element_type=F32)
    grad = nodes[:, :128].reshape(3, 8, 8, 128)
    hess = nodes[:, 128:].reshape(3, 8, 8, 128)
    upper = lax.broadcasted_iota(jnp.int32, (8, 128), 1) >= 64

    def score(g, h):
        return g * g / (h + reg)

    for p in range(3):
        g_all, h_all = grad[p, 7], hess[p, 7]
        g_all = jnp.where(upper, g_all, pltpu.roll(g_all, 64, 1))
        h_all = jnp.where(upper, h_all, pltpu.roll(h_all, 64, 1))
        whole = score(g_all, h_all)
        for q in range(8):
            g_left, h_left = grad[p, q], hess[p, q]
            gain = 0.5 * (score(g_left, h_left) + score(g_all - g_left, h_all - h_left) - whole)
            gain_ref[2 * q, pl.ds(8 * p, 8), :] = gain[:, :63]
            if q < 7:
                gain_ref[2 * q + 1, pl.ds(8 * p, 8), :] = pltpu.roll(gain, 64, 1)[:, :63]
    last = sums_ref[0, 1, 1, 1]
    g_leaf, h_leaf = pltpu.roll(last, 64, 1), pltpu.roll(last, 32, 1)
    leaf_ref[...] = (-g_leaf / (h_leaf + reg))[0:1, :LEAVES]
    lanes = lax.broadcasted_iota(jnp.int32, (1, 128), 1)
    steps = lax.broadcasted_iota(jnp.int32, (BINS - 1, 128), 0)
    value = jnp.zeros((1, 128), F32)
    for j in range(INNER):
        feat = feat_ref[j]
        tile = cut_ref[:, pl.ds(pl.multiple_of(feat // 128 * 128, 128), 128)]
        one = jnp.sum(jnp.where(steps == thr_ref[j], tile, 0.0), axis=0, keepdims=True)
        one = jnp.sum(jnp.where(lanes == feat % 128, one, 0.0), axis=1, keepdims=True)
        value = jnp.where(lanes == j, one, value)
    value_ref[...] = value[:, :INNER]


def solution(mesh):
    row_spec = P(('trees', 'data'))
    vmem = pl.BlockSpec(memory_space=pltpu.VMEM)
    smem = pl.BlockSpec(memory_space=pltpu.SMEM)
    hbm = pl.BlockSpec(memory_space=pl.ANY)

    def device_fn(bin_codes, gradient, hessian, valid_rows, split_feat, split_thr, cut_values, reg_lambda):
        sums = pl.pallas_call(
            hist_kernel,
            out_shape=jax.ShapeDtypeStruct((3, 2, 2, 2, 8, 128), F32),
            in_specs=[hbm, vmem, vmem, smem, smem, smem],
            out_specs=vmem,
            scratch_shapes=[
                pltpu.VMEM((LOADS, ROWS, SLAB), jnp.int32),
                pltpu.VMEM((64, 2, 24, ROWS), F32),
                pltpu.VMEM((64, 24, ROWS), F32),
                pltpu.VMEM((3, 4, 4, 4, 16, 2 * ROWS), BF16),
                pltpu.VMEM((2, 8, ROWS), F32),
                pltpu.VMEM((2 * ROWS, 256), BF16),
                pltpu.VMEM((3, 2, 4, 2, 4, 8, 8, 128), F32),
                pltpu.VMEM((3, 2, 3, 2, 4, 8, 8, 128), F32),
                pltpu.VMEM((3, 2, 3, 2, 8, 8, 128), F32),
                pltpu.VMEM((3, 2, 3, 2, 2, 8, 128), F32),
                pltpu.SemaphoreType.DMA((LOADS,)),
                pltpu.SemaphoreType.DMA((LOADS + 1,)),
                pltpu.SemaphoreType.DMA((LOADS + 1,)),
                pltpu.SemaphoreType.DMA((108,)),
                pltpu.SemaphoreType.DMA((108,)),
            ],
            compiler_params=pltpu.CompilerParams(collective_id=0, has_side_effects=True, vmem_limit_bytes=60 * 1024 * 1024),
            name='hist',
        )(bin_codes, gradient.reshape(1, ROWS), hessian.reshape(1, ROWS), valid_rows, split_feat, split_thr)
        gain, leaf, value = pl.pallas_call(
            gain_kernel,
            out_shape=(jax.ShapeDtypeStruct((BINS - 1, FEATS // 128, 63), F32), jax.ShapeDtypeStruct((1, LEAVES), F32), jax.ShapeDtypeStruct((1, INNER), F32)),
            in_specs=[vmem, vmem, smem, smem, smem],
            out_specs=(vmem, vmem, vmem),
            name='gain',
        )(sums, cut_values.T, split_feat, split_thr, reg_lambda)
        return jnp.transpose(gain, (2, 1, 0)), leaf.reshape(LEAVES), value.reshape(INNER)

    return jax.shard_map(device_fn, mesh=mesh, in_specs=(P(('trees', 'data'), None), row_spec, row_spec, row_spec, P('trees'), P('trees'), P('trees', None), P('trees')), out_specs=(P(None, ('trees', 'data'), None), P('trees'), P('trees')), check_vma=False)
```

time: 342 us -> 63.3 us (0.19)
  the two profiles are of different devices: /device:TPU:1 before, /device:TPU:0 now
where the time goes in v2:
time: 63.3 us; the launch traced here: 63.1 us
  Pallas kernels  61.2 us (97%)
  between operations  1.93 us (3%)
    pallas_call x1, Pallas kernels, device_fn(): pl.pallas_call(hist_kernel, out_shape=jax.ShapeDtypeStruct((3, 2, 2, 2, 8...  58.9 us
    pallas_call x1, Pallas kernels, device_fn(): pl.pallas_call(gain_kernel, out_shape=(jax.ShapeDtypeStruct((BINS - 1, FE...  2.31 us

profile of v2, /device:TPU:0, one launch (start us, length us, event | category | flops | bytes accessed | tf_op | source)
XLA Modules:
  0.0 63.1 jit_solution(10354630255863579524)
XLA Ops:
  1.9 58.9 %hist.1.sums_ref = f32[3,2,2,2,8,128]{5,4,3,2,1,0:T(8,128)} custom-call(s32[512,3072]{1,0:T(8,128)} %codes_hbm.1, f32[1,512]{1,0:T(1,128)} %bitcast.7, f32[1,512]{1,0:T(1,128)} %bitcast.8, s32[1]{0:T(128)S(6)} %copy.11.valid_ref, s32[31]{0:T(128)} %feat_ref.3, s32[31]{0:T(128)} %thr_ref.3), custom_call_target="tpu_custom_call" | custom-call | tf_op jit(solution)/shard_map/hist/pallas_call | solution.py:314
  60.8 2.3 %gain.1 = (f32[15,24,63]{2,1,0:T(8,128)}, f32[1,32]{1,0:T(1,128)}, f32[1,31]{1,0:T(1,128)}) custom-call(f32[3,2,2,2,8,128]{5,4,3,2,1,0:T(8,128)} %hist.1.sums_ref, f32[15,3072]{1,0:T(8,128)} %bitcast.6, s32[31]{0:T(128)} %feat_ref.3, s32[31]{0:T(128)} %thr_ref.3, f32[1]{0:T(128)S(6)} %copy.12.reg_ref), custom_call_target="tpu_custom_call" | custom-call | tf_op jit(solution)/shard_map/gain/pallas_call | solution.py:339

commit v3 on v2

v3 whole, which is shorter than its diff:
```python
import functools
import jax
import jax.numpy as jnp
from jax import lax
from jax.experimental import pallas as pl
from jax.experimental.pallas import tpu as pltpu
from jax.sharding import PartitionSpec as P

F32 = jnp.float32
BF16 = jnp.bfloat16
ROWS = 512
FEATS = 3072
BINS = 16
LEAVES = 32
INNER = 31
LOADS = 8
SLAB = FEATS // LOADS


def pow4(dim):
    return 1 + 3 * dim * (3 * dim - 1) // 2


def coord(me, dim):
    return (me // 2) // pow4(dim) % 4


def neighbour(me, dim, step):
    at = coord(me, dim)
    return me + ((at + step + 4) % 4 - at) * 2 * pow4(dim)


def hist_kernel(codes_hbm, grad_ref, hess_ref, valid_ref, feat_ref, thr_ref, cut_hbm, out_ref, value_ref,
                raw, turned, turned_rx, codes2, meta, weights, cuts, hist, rx1, rx2, rx3,
                load_sem, pair_send, pair_recv, send_sem, recv_sem):
    me = lax.axis_index('data')
    core = me % 2
    partner = me + 1 - 2 * core

    def remote(src, dst, s_sem, r_sem, device):
        return pltpu.make_async_remote_copy(src_ref=src, dst_ref=dst, send_sem=s_sem, recv_sem=r_sem, device_id=(0, device), device_id_type=pl.DeviceIdType.MESH)

    def load(m):
        return pltpu.make_async_copy(codes_hbm.at[:, pl.ds(m * SLAB, SLAB)], raw.at[m], load_sem.at[m])

    for m in range(LOADS):
        load(m).start()
    barrier = pltpu.get_barrier_semaphore()
    pl.semaphore_signal(barrier, inc=1, device_id=(0, partner), device_id_type=pl.DeviceIdType.MESH)
    for dim in range(3):
        for step in (1, 2, 3):
            pl.semaphore_signal(barrier, inc=1, device_id=(0, neighbour(me, dim, step)), device_id_type=pl.DeviceIdType.MESH)
    pl.semaphore_wait(barrier, 10)

    def pair_copy(m):
        return remote(turned.at[pl.ds(m * 8, 8), 1 - core], turned_rx.at[pl.ds(m * 8, 8)], pair_send.at[0], pair_recv.at[m], partner)

    meta_copy = remote(meta.at[0], meta.at[1], pair_send.at[1], pair_recv.at[LOADS], partner)

    def fill_codes(source, lane0, chip):
        where = (chip % 4, chip // 4 % 4, chip // 16)
        for p in range(3):
            v = source(p)
            codes2[p, where[p], where[(p + 1) % 3], where[(p + 2) % 3], :, pl.ds(lane0, ROWS)] = jnp.concatenate([v, v - 1.0], axis=0).astype(BF16)

    def fill_own(m):
        for k in range(8):
            chip = m * 8 + k
            fill_codes(lambda p: turned[chip, core, pl.ds(8 * p, 8), :], 0, chip)

    def turn(m):
        block = raw[m].astype(F32).astype(BF16)
        turned[pl.ds(m * 8, 8)] = block.T.astype(F32).reshape(8, 2, 24, ROWS)

    load(0).wait()
    turn(0)
    pair_copy(0).start()

    @pl.loop(1, LOADS)
    def _(m):
        load(m).wait()
        fill_own(m - 1)
        turn(m)
        pair_copy(m).start()

    @pl.loop(0, FEATS // 128)
    def _(k):
        pltpu.make_async_copy(cut_hbm.at[:, pl.ds(k * 128, 128)], cuts.at[k], load_sem.at[LOADS]).start()

    fill_own(LOADS - 1)

    def goes_right(j):
        feat = feat_ref[j]
        column = turned[feat // 48, feat // 24 % 2, pl.ds(feat % 24, 1), :]
        return (column > thr_ref[j].astype(F32)).astype(jnp.int32)

    leaf = goes_right(0)
    for level in range(1, 5):
        width = 2 ** level
        bit = goes_right(width - 1)
        for n in range(1, width):
            bit = jnp.where(leaf == n, goes_right(width - 1 + n), bit)
        leaf = 2 * leaf + bit
    live = lax.broadcasted_iota(jnp.int32, (1, ROWS), 1) < valid_ref[0]
    grad = jnp.where(live, grad_ref[...], 0.0)
    hess = jnp.where(live, hess_ref[...], 0.0)
    meta[0] = jnp.concatenate([grad, hess, leaf.astype(F32), jnp.zeros((5, ROWS), F32)], axis=0)
    meta_copy.start()

    def split3(v):
        hi = v.astype(BF16).astype(F32)
        mid = (v - hi).astype(BF16).astype(F32)
        return hi, mid, v - hi - mid

    def fill_weights(side):
        for k in range(ROWS // 128):
            lanes = pl.ds(k * 128, 128)
            g3 = split3(meta[side, 0:1, lanes])
            h3 = split3(meta[side, 1:2, lanes])
            hit = meta[side, 2:3, lanes] == lax.broadcasted_iota(jnp.int32, (LEAVES, 128), 0).astype(F32)
            rows = []
            for i in range(3):
                rows.append(jnp.where(hit, g3[i], 0.0))
                rows.append(jnp.where(hit, h3[i], 0.0))
            rows.append(jnp.zeros((64, 128), F32))
            weights[pl.ds(side * ROWS + k * 128, 128), :] = jnp.concatenate(rows, axis=0).T.astype(BF16)

    fill_weights(0)

    def block(ph, c, p, half, j):
        if ph == 0:
            return hist.at[p, c, j, half]
        return hist.at[p, c, coord(me, p), half, j]

    landings = (rx1, rx2)

    def copy(ph, c, p, kind, half):
        dim = (p + ph) % 3
        at = coord(me, dim)
        step = 1 if (kind == 1) == (half == 1) else -1
        j = (at + 2) % 4 if kind == 0 else (at + step + 4) % 4
        s = ((ph * 2 + c) * 3 + p) * 2 + (0 if kind == 0 else 1)
        return remote(block(ph, c, p, half, j), landings[ph].at[p, c, kind, half], send_sem.at[ph], recv_sem.at[s], neighbour(me, dim, step))

    def wait_landed(ph, c, p, kind, count):
        s = ((ph * 2 + c) * 3 + p) * 2 + (0 if kind == 0 else 1)
        place = landings[ph].at[p, c, pl.ds(kind, count)]
        remote(place, place, send_sem.at[ph], recv_sem.at[s], partner).wait_recv()

    def send_far(ph, c, p):
        copy(ph, c, p, 0, 0).start()
        copy(ph, c, p, 0, 1).start()

    def send_near(ph, c, p):
        copy(ph, c, p, 1, 1).start()
        copy(ph, c, p, 1, 0).start()

    def relay(ph, c, p):
        at = coord(me, (p + ph) % 3)
        wait_landed(ph, c, p, 0, 1)
        for half in range(2):
            mine = block(ph, c, p, half, (at + (1, 3)[half]) % 4)
            mine[...] = mine[...] + landings[ph][p, c, 0, half]
            copy(ph, c, p, 2, half).start()

    def collect(ph, c, p):
        at = coord(me, (p + ph) % 3)
        wait_landed(ph, c, p, 1, 2)
        for half in range(2):
            mine = block(ph, c, p, half, at)
            total = mine[...] + landings[ph][p, c, 1, half] + landings[ph][p, c, 2, half]
            mine[...] = total
        if ph == 0:
            send_far(1, c, p)
            send_near(1, c, p)
        else:
            for step in (2, 1, 3):
                last_copy(c, p, step).start()

    def last_block(c, p, j):
        return hist.at[p, c, coord(me, p), :, coord(me, (p + 1) % 3), pl.ds(2 * j, 2)]

    def last_copy(c, p, step):
        dim = (p + 2) % 3
        j = (coord(me, dim) + step) % 4
        return remote(last_block(c, p, j), rx3.at[p, c, step - 1], send_sem.at[2], recv_sem.at[24 + 3 * c + p], neighbour(me, dim, step))

    def last_collect(c, p):
        remote(rx3.at[p, c], rx3.at[p, c], send_sem.at[2], recv_sem.at[24 + 3 * c + p], partner).wait_recv()
        out_ref[p, c] = last_block(c, p, coord(me, (p + 2) % 3))[...] + rx3[p, c, 0] + rx3[p, c, 1] + rx3[p, c, 2]

    first_half = lax.broadcasted_iota(jnp.int32, (64, 8, 128), 2) < 64

    def unit(c, p, jj, lane0, lanes, add):
        ahead = (2 + 3 * jj + (jj // 2) * (7 - 2 * jj)) % 4
        ja = (coord(me, p) + ahead) % 4
        bounds = [jnp.full((16, lanes), (8 * c + 2 * k).astype(F32), F32).astype(BF16) for k in range(4)]
        one = jnp.asarray(1, BF16)
        zero = jnp.asarray(0, BF16)
        pieces = []
        for half in range(2):
            for jb in range(4):
                for jc in range(4):
                    code = codes2[p, ja, jb, jc, :, pl.ds(lane0, lanes)]
                    for q in range(2):
                        pieces.append(jnp.where(code <= bounds[half * 2 + q], one, zero))
        left = jnp.concatenate(pieces, axis=0)
        sums = jnp.dot(left, weights[pl.ds(lane0, lanes), :], preferred_element_type=F32)
        sums = (sums[:, :128] + sums[:, 128:]).reshape(64, 2, 8, 128)
        even, odd = sums[:, 0], sums[:, 1]
        keep = jnp.where(first_half, even, odd)
        turn = jnp.where(first_half, odd, even).reshape(512, 128)
        both = (keep + pltpu.roll(turn, 64, 1).reshape(64, 8, 128)).reshape(2, 4, 8, 8, 128)
        if add:
            both = both + hist[p, c, ja]
        hist[p, c, ja] = both

    zero_c = jnp.int32(0)

    @pl.loop(0, 2)
    def _(jj):
        for p in range(3):
            unit(zero_c, p, jj, 0, ROWS, False)

    @pl.loop(0, LOADS)
    def _(m):
        pair_copy(m).wait_recv()
        for k in range(8):
            chip = m * 8 + k
            fill_codes(lambda p: turned_rx[chip, pl.ds(8 * p, 8), :], ROWS, chip)

    meta_copy.wait_recv()
    fill_weights(1)

    def for_parts(task, *args):
        for p in range(3):
            task(*args, p)

    @pl.loop(0, 2)
    def _(jj):
        for p in range(3):
            unit(zero_c, p, jj, ROWS, ROWS, True)

        @pl.when(jj == 0)
        def _():
            for_parts(send_far, 0, 0)

        @pl.when(jj == 1)
        def _():
            for p in range(3):
                copy(0, 0, p, 1, 1).start()

    @pl.loop(2, 8)
    def _(b):
        c, jj = b // 4, b % 4
        for p in range(3):
            unit(c, p, jj, 0, 2 * ROWS, False)

        @pl.when(jj == 0)
        def _():
            for_parts(send_far, 0, c)

        @pl.when(jj == 1)
        def _():
            for p in range(3):
                copy(0, c, p, 1, 1).start()

        @pl.when(jj == 2)
        def _():
            for p in range(3):
                copy(0, c, p, 1, 0).start()

        @pl.when(b == 3)
        def _():
            for_parts(relay, 0, 0)

        @pl.when(b == 6)
        def _():
            for_parts(collect, 0, 0)

    for_parts(relay, 0, 1)

    pltpu.make_async_copy(cuts, cuts, load_sem.at[LOADS]).wait()
    lanes = lax.broadcasted_iota(jnp.int32, (1, 128), 1)
    steps = lax.broadcasted_iota(jnp.int32, (BINS - 1, 128), 0)
    value = jnp.zeros((1, 128), F32)
    for j in range(INNER):
        feat = feat_ref[j]
        one = jnp.sum(jnp.where(steps == thr_ref[j], cuts[feat // 128], 0.0), axis=0, keepdims=True)
        one = jnp.sum(jnp.where(lanes == feat % 128, one, 0.0), axis=1, keepdims=True)
        value = jnp.where(lanes == j, one, value)
    value_ref[...] = value

    for_parts(relay, 1, 0)
    for_parts(collect, 0, 1)
    for_parts(collect, 1, 0)
    for_parts(relay, 1, 1)
    for_parts(last_collect, 0)
    for_parts(collect, 1, 1)
    for_parts(last_collect, 1)

    meta_copy.wait_send()
    remote(turned_rx, turned_rx, pair_send.at[0], pair_recv.at[0], partner).wait_send()
    for ph, place in enumerate((rx1, rx2, rx3)):
        remote(place, place, send_sem.at[ph], recv_sem.at[0], partner).wait_send()


def gain_kernel(sums_ref, found_ref, reg_ref, gain_ref, leaf_ref, value_ref):
    reg = reg_ref[0]
    sums = sums_ref[...].reshape(192, 128)
    lane = lax.broadcasted_iota(jnp.int32, (128, 256), 0)
    col = lax.broadcasted_iota(jnp.int32, (128, 256), 1)
    same = (lane // 64 == col // 64 % 2) & (lane // 32 % 2 == col // 128)
    under = lane % 32 + 32
    hit = under == col % 64 + 1
    for _ in range(5):
        under = under // 2
        hit = hit | (under == col % 64 + 1)
    pick = jnp.where(same & hit, 1.0, 0.0).astype(BF16)
    hi = sums.astype(BF16)
    rest = sums - hi.astype(F32)
    mid = rest.astype(BF16)
    low = (rest - mid.astype(F32)).astype(BF16)
    nodes = jnp.dot(low, pick, preferred_element_type=F32) + jnp.dot(mid, pick, preferred_element_type=F32) + jnp.dot(hi, pick, preferred_element_type=F32)
    grad = nodes[:, :128].reshape(3, 8, 8, 128)
    hess = nodes[:, 128:].reshape(3, 8, 8, 128)
    upper = lax.broadcasted_iota(jnp.int32, (8, 128), 1) >= 64

    def score(g, h):
        return g * g / (h + reg)

    for p in range(3):
        g_all, h_all = grad[p, 7], hess[p, 7]
        g_all = jnp.where(upper, g_all, pltpu.roll(g_all, 64, 1))
        h_all = jnp.where(upper, h_all, pltpu.roll(h_all, 64, 1))
        whole = score(g_all, h_all)
        for q in range(8):
            g_left, h_left = grad[p, q], hess[p, q]
            gain = 0.5 * (score(g_left, h_left) + score(g_all - g_left, h_all - h_left) - whole)
            gain_ref[2 * q, pl.ds(8 * p, 8), :] = gain[:, :63]
            if q < 7:
                gain_ref[2 * q + 1, pl.ds(8 * p, 8), :] = pltpu.roll(gain, 64, 1)[:, :63]
    last = sums_ref[0, 1, 1, 1]
    g_leaf, h_leaf = pltpu.roll(last, 64, 1), pltpu.roll(last, 32, 1)
    leaf_ref[...] = (-g_leaf / (h_leaf + reg))[0:1, :LEAVES]
    value_ref[...] = found_ref[:, :INNER]


def solution(mesh):
    row_spec = P(('trees', 'data'))
    vmem = pl.BlockSpec(memory_space=pltpu.VMEM)
    smem = pl.BlockSpec(memory_space=pltpu.SMEM)
    hbm = pl.BlockSpec(memory_space=pl.ANY)

    def device_fn(bin_codes, gradient, hessian, valid_rows, split_feat, split_thr, cut_values, reg_lambda):
        sums, found = pl.pallas_call(
            hist_kernel,
            out_shape=(jax.ShapeDtypeStruct((3, 2, 2, 2, 8, 128), F32), jax.ShapeDtypeStruct((1, 128), F32)),
            in_specs=[hbm, vmem, vmem, smem, smem, smem, hbm],
            out_specs=(vmem, vmem),
            scratch_shapes=[
                pltpu.VMEM((LOADS, ROWS, SLAB), jnp.int32),
                pltpu.VMEM((64, 2, 24, ROWS), F32),
                pltpu.VMEM((64, 24, ROWS), F32),
                pltpu.VMEM((3, 4, 4, 4, 16, 2 * ROWS), BF16),
                pltpu.VMEM((2, 8, ROWS), F32),
                pltpu.VMEM((2 * ROWS, 256), BF16),
                pltpu.VMEM((FEATS // 128, BINS - 1, 128), F32),
                pltpu.VMEM((3, 2, 4, 2, 4, 8, 8, 128), F32),
                pltpu.VMEM((3, 2, 3, 2, 4, 8, 8, 128), F32),
                pltpu.VMEM((3, 2, 3, 2, 8, 8, 128), F32),
                pltpu.VMEM((3, 2, 3, 2, 2, 8, 128), F32),
                pltpu.SemaphoreType.DMA((LOADS + 1,)),
                pltpu.SemaphoreType.DMA((2,)),
                pltpu.SemaphoreType.DMA((LOADS + 1,)),
                pltpu.SemaphoreType.DMA((3,)),
                pltpu.SemaphoreType.DMA((30,)),
            ],
            compiler_params=pltpu.CompilerParams(collective_id=0, has_side_effects=True, vmem_limit_bytes=60 * 1024 * 1024),
            name='hist',
        )(bin_codes, gradient.reshape(1, ROWS), hessian.reshape(1, ROWS), valid_rows, split_feat, split_thr, cut_values.T)
        gain, leaf, value = pl.pallas_call(
            gain_kernel,
            out_shape=(jax.ShapeDtypeStruct((BINS - 1, FEATS // 128, 63), F32), jax.ShapeDtypeStruct((1, LEAVES), F32), jax.ShapeDtypeStruct((1, INNER), F32)),
            in_specs=[vmem, vmem, smem],
            out_specs=(vmem, vmem, vmem),
            compiler_params=pltpu.CompilerParams(vmem_limit_bytes=4 * 1024 * 1024),
            name='gain',
        )(sums, found, reg_lambda)
        return jnp.transpose(gain, (2, 1, 0)), leaf.reshape(LEAVES), value.reshape(INNER)

    return jax.shard_map(device_fn, mesh=mesh, in_specs=(P(('trees', 'data'), None), row_spec, row_spec, row_spec, P('trees'), P('trees'), P('trees', None), P('trees')), out_specs=(P(None, ('trees', 'data'), None), P('trees'), P('trees')), check_vma=False)
```

time: 63.3 us -> 53.4 us (0.84)
  Pallas kernels: 61.2 us -> 49.7 us
  local copies, waits for them, and re-layouts: 0 us -> 1.54 us
    pallas_call x1, Pallas kernels: 58.9 us -> 48.4 us  [device_fn(): pl.pallas_call(hist_kernel, out_shape=(jax.ShapeDtypeStruct((3, 2, 2, 2,...]
    unnamed x0 -> x4, local copies, waits for them, and re-layouts: none -> 1.54 us
    pallas_call x1, Pallas kernels: 2.31 us -> 1.27 us  [device_fn(): pl.pallas_call(gain_kernel, out_shape=(jax.ShapeDtypeStruct((BINS - 1, FE...]
where the time goes in v3:
time: 53.4 us; the launch traced here: 53.2 us
  Pallas kernels  49.7 us (93%)
  between operations  1.94 us (4%)
  local copies, waits for them, and re-layouts  1.54 us (3%)
    pallas_call x1, Pallas kernels, device_fn(): pl.pallas_call(hist_kernel, out_shape=(jax.ShapeDtypeStruct((3, 2, 2, 2,...  48.4 us
    unnamed x4, local copies, waits for them, and re-layouts  1.54 us
    pallas_call x1, Pallas kernels, device_fn(): pl.pallas_call(gain_kernel, out_shape=(jax.ShapeDtypeStruct((BINS - 1, FE...  1.27 us

profile of v3, /device:TPU:0, one launch (start us, length us, event | category | flops | bytes accessed | tf_op | source)
XLA Modules:
  0.0 53.2 jit_solution(8124548074562836722)
XLA Ops:
  1.9 48.4 %hist.1 = (f32[3,2,2,2,8,128]{5,4,3,2,1,0:T(8,128)}, f32[1,128]{1,0:T(1,128)}) custom-call(s32[512,3072]{1,0:T(8,128)} %codes_hbm.1, f32[1,512]{1,0:T(1,128)} %bitcast.7, f32[1,512]{1,0:T(1,128)} %bitcast.8, s32[1]{0:T(128)S(6)} %copy.11.valid_ref, s32[31]{0:T(128)} %feat_ref.1, s32[31]{0:T(128)} %thr_ref.1, f32[15,3072]{1,0:T(8,128)} %bitcast.6), custom_call_target="tpu_custom_call" | custom-call | tf_op jit(solution)/shard_map/hist/pallas_call | solution.py:356
  50.4 0.0 copy-start
  50.4 0.9 %copy-done = f32[3,2,2,2,8,128]{5,4,3,2,1,0:T(8,128)S(1)} copy-done((f32[3,2,2,2,8,128]{5,4,3,2,1,0:T(8,128)S(1)}, f32[3,2,2,2,8,128]{5,4,3,2,1,0:T(8,128)}, u32[]{:S(2)}) %copy-start) | copy-done | bytes 98328
  51.2 0.0 copy-start.1
  51.3 0.7 %copy-done.1 = f32[1,128]{1,0:T(1,128)S(1)} copy-done((f32[1,128]{1,0:T(1,128)S(1)}, f32[1,128]{1,0:T(1,128)}, u32[]{:S(2)}) %copy-start.1) | copy-done | bytes 536
  51.9 1.3 %gain.1 = (f32[15,24,63]{2,1,0:T(8,128)}, f32[1,32]{1,0:T(1,128)}, f32[1,31]{1,0:T(1,128)}) custom-call(f32[3,2,2,2,8,128]{5,4,3,2,1,0:T(8,128)S(1)} %copy-done, f32[1,128]{1,0:T(1,128)S(1)} %copy-done.1, f32[1]{0:T(128)S(6)} %copy.12.reg_ref), custom_call_target="tpu_custom_call" | custom-call | tf_op jit(solution)/shard_map/gain/pallas_call | solution.py:382
Async XLA Ops:
  50.4 0.9 %copy-start = (f32[3,2,2,2,8,128]{5,4,3,2,1,0:T(8,128)S(1)}, f32[3,2,2,2,8,128]{5,4,3,2,1,0:T(8,128)}, u32[]{:S(2)}) copy-start(f32[3,2,2,2,8,128]{5,4,3,2,1,0:T(8,128)} %get-tuple-element.8.sums_ref) | copy-start | bytes 294916
  51.2 0.7 %copy-start.1 = (f32[1,128]{1,0:T(1,128)S(1)}, f32[1,128]{1,0:T(1,128)}, u32[]{:S(2)}) copy-start(f32[1,128]{1,0:T(1,128)} %get-tuple-element.9.found_ref) | copy-start | bytes 1540

commit v4 on v3

--- a/solution.py
+++ b/solution.py
@@ -30,8 +30,8 @@
     return me + ((at + step + 4) % 4 - at) * 2 * pow4(dim)
 
 
-def hist_kernel(codes_hbm, grad_ref, hess_ref, valid_ref, feat_ref, thr_ref, cut_hbm, out_ref, value_ref,
-                raw, turned, turned_rx, codes2, meta, weights, cuts, hist, rx1, rx2, rx3,
+def hist_kernel(codes_hbm, grad_hbm, hess_hbm, valid_hbm, feat_hbm, thr_hbm, cut_hbm, reg_hbm, out_ref, value_ref,
+                grad_ref, hess_ref, valid_ref, feat_ref, thr_ref, reg_ref, raw, turned, turned_rx, codes2, meta, weights, cuts, hist, rx1, rx2, rx3,
                 load_sem, pair_send, pair_recv, send_sem, recv_sem):
     me = lax.axis_index('data')
     core = me % 2
@@ -45,6 +45,10 @@
 
     for m in range(LOADS):
         load(m).start()
+    small = [pltpu.make_async_copy(src, dst, load_sem.at[LOADS + 1 + k]) for k, (src, dst) in enumerate(
+        ((grad_hbm, grad_ref), (hess_hbm, hess_ref), (valid_hbm, valid_ref), (feat_hbm, feat_ref), (thr_hbm, thr_ref), (reg_hbm, reg_ref)))]
+    for one in small:
+        one.start()
     barrier = pltpu.get_barrier_semaphore()
     pl.semaphore_signal(barrier, inc=1, device_id=(0, partner), device_id_type=pl.DeviceIdType.MESH)
     for dim in range(3):
@@ -52,36 +56,61 @@
             pl.semaphore_signal(barrier, inc=1, device_id=(0, neighbour(me, dim, step)), device_id_type=pl.DeviceIdType.MESH)
     pl.semaphore_wait(barrier, 10)
 
-    def pair_copy(m):
-        return remote(turned.at[pl.ds(m * 8, 8), 1 - core], turned_rx.at[pl.ds(m * 8, 8)], pair_send.at[0], pair_recv.at[m], partner)
-
-    meta_copy = remote(meta.at[0], meta.at[1], pair_send.at[1], pair_recv.at[LOADS], partner)
-
-    def fill_codes(source, lane0, chip):
-        where = (chip % 4, chip // 4 % 4, chip // 16)
+    def ahead(jj):
+        return (2 + 3 * jj + (jj // 2) * (7 - 2 * jj)) % 4
+
+    def pair_copy(jj, p):
+        ja = (coord(me, p) + ahead(jj)) % 4
+        other = 1 - core
+        rows = pl.ds(8 * p, 8)
+        if p == 0:
+            src, dst = turned.at[:, :, ja, other, rows], turned_rx.at[:, :, ja, rows]
+        elif p == 1:
+            src, dst = turned.at[:, ja, :, other, rows], turned_rx.at[:, ja, :, rows]
+        else:
+            src, dst = turned.at[ja, :, :, other, rows], turned_rx.at[ja, :, :, rows]
+        return remote(src, dst, pair_send.at[0], pair_recv.at[jj], partner)
+
+    meta_copy = remote(meta.at[0], meta.at[1], pair_send.at[1], pair_recv.at[4], partner)
+
+    def put_code(p, ja, jb, jc, lane0, v):
+        codes2[p, ja, jb, jc, :, pl.ds(lane0, ROWS)] = jnp.concatenate([v, v - 1.0], axis=0).astype(BF16)
+
+    def fill_own(m):
+        z = m // 2
+        for k in range(8):
+            y, x = m % 2 * 2 + k // 4, k % 4
+            for p in range(3):
+                at = ((x, y, z), (y, z, x), (z, x, y))[p]
+                put_code(p, *at, 0, turned[z, y, x, core, pl.ds(8 * p, 8), :])
+
+    def fill_other(jj):
         for p in range(3):
-            v = source(p)
-            codes2[p, where[p], where[(p + 1) % 3], where[(p + 2) % 3], :, pl.ds(lane0, ROWS)] = jnp.concatenate([v, v - 1.0], axis=0).astype(BF16)
-
-    def fill_own(m):
-        for k in range(8):
-            chip = m * 8 + k
-            fill_codes(lambda p: turned[chip, core, pl.ds(8 * p, 8), :], 0, chip)
+            ja = (coord(me, p) + ahead(jj)) % 4
+            for jb in range(4):
+                for jc in range(4):
+                    z, y, x = ((jc, jb, ja), (jb, ja, jc), (ja, jc, jb))[p]
+                    put_code(p, ja, jb, jc, ROWS, turned_rx[z, y, x, pl.ds(8 * p, 8), :])
+
+    def other_codes(jj):
+        remote(turned_rx.at[0], turned_rx.at[0], pair_send.at[0], pair_recv.at[jj], partner).wait_recv()
+        fill_other(jj)
 
     def turn(m):
         block = raw[m].astype(F32).astype(BF16)
-        turned[pl.ds(m * 8, 8)] = block.T.astype(F32).reshape(8, 2, 24, ROWS)
+        turned[m // 2, pl.ds(m % 2 * 2, 2)] = block.T.astype(F32).reshape(2, 4, 2, 24, ROWS)
 
     load(0).wait()
     turn(0)
-    pair_copy(0).start()
 
     @pl.loop(1, LOADS)
     def _(m):
         load(m).wait()
         fill_own(m - 1)
         turn(m)
-        pair_copy(m).start()
+
+    for p in range(3):
+        pair_copy(0, p).start()
 
     @pl.loop(0, FEATS // 128)
     def _(k):
@@ -89,9 +118,12 @@
 
     fill_own(LOADS - 1)
 
+    for one in small:
+        one.wait()
+
     def goes_right(j):
         feat = feat_ref[j]
-        column = turned[feat // 48, feat // 24 % 2, pl.ds(feat % 24, 1), :]
+        column = turned[feat // 768, feat // 192 % 4, feat // 48 % 4, feat // 24 % 2, pl.ds(feat % 24, 1), :]
         return (column > thr_ref[j].astype(F32)).astype(jnp.int32)
 
     leaf = goes_right(0)
@@ -101,11 +133,14 @@
         for n in range(1, width):
             bit = jnp.where(leaf == n, goes_right(width - 1 + n), bit)
         leaf = 2 * leaf + bit
-    live = lax.broadcasted_iota(jnp.int32, (1, ROWS), 1) < valid_ref[0]
+    live = lax.broadcasted_iota(jnp.int32, (1, ROWS), 1) < valid_ref[...]
     grad = jnp.where(live, grad_ref[...], 0.0)
     hess = jnp.where(live, hess_ref[...], 0.0)
     meta[0] = jnp.concatenate([grad, hess, leaf.astype(F32), jnp.zeros((5, ROWS), F32)], axis=0)
     meta_copy.start()
+    for jj in range(1, 4):
+        for p in range(3):
+            pair_copy(jj, p).start()
 
     def split3(v):
         hi = v.astype(BF16).astype(F32)
@@ -192,8 +227,7 @@
     first_half = lax.broadcasted_iota(jnp.int32, (64, 8, 128), 2) < 64
 
     def unit(c, p, jj, lane0, lanes, add):
-        ahead = (2 + 3 * jj + (jj // 2) * (7 - 2 * jj)) % 4
-        ja = (coord(me, p) + ahead) % 4
+        ja = (coord(me, p) + ahead(jj)) % 4
         bounds = [jnp.full((16, lanes), (8 * c + 2 * k).astype(F32), F32).astype(BF16) for k in range(4)]
         one = jnp.asarray(1, BF16)
         zero = jnp.asarray(0, BF16)
@@ -215,20 +249,10 @@
             both = both + hist[p, c, ja]
         hist[p, c, ja] = both
 
-    zero_c = jnp.int32(0)
-
-    @pl.loop(0, 2)
-    def _(jj):
-        for p in range(3):
-            unit(zero_c, p, jj, 0, ROWS, False)
-
-    @pl.loop(0, LOADS)
-    def _(m):
-        pair_copy(m).wait_recv()
-        for k in range(8):
-            chip = m * 8 + k
-            fill_codes(lambda p: turned_rx[chip, pl.ds(8 * p, 8), :], ROWS, chip)
-
+    zero = jnp.int32(0)
+    for p in range(3):
+        unit(zero, p, 0, 0, ROWS, False)
+    other_codes(0)
     meta_copy.wait_recv()
     fill_weights(1)
 
@@ -236,23 +260,18 @@
         for p in range(3):
             task(*args, p)
 
-    @pl.loop(0, 2)
-    def _(jj):
-        for p in range(3):
-            unit(zero_c, p, jj, ROWS, ROWS, True)
-
-        @pl.when(jj == 0)
-        def _():
-            for_parts(send_far, 0, 0)
-
-        @pl.when(jj == 1)
-        def _():
-            for p in range(3):
-                copy(0, 0, p, 1, 1).start()
-
-    @pl.loop(2, 8)
+    for p in range(3):
+        unit(zero, p, 0, ROWS, ROWS, True)
+    for_parts(send_far, 0, 0)
+
+    @pl.loop(1, 8)
     def _(b):
         c, jj = b // 4, b % 4
+
+        @pl.when(c == 0)
+        def _():
+            other_codes(jj)
+
         for p in range(3):
             unit(c, p, jj, 0, 2 * ROWS, False)
 
@@ -289,7 +308,7 @@
         one = jnp.sum(jnp.where(steps == thr_ref[j], cuts[feat // 128], 0.0), axis=0, keepdims=True)
         one = jnp.sum(jnp.where(lanes == feat % 128, one, 0.0), axis=1, keepdims=True)
         value = jnp.where(lanes == j, one, value)
-    value_ref[...] = value
+    value_ref[...] = jnp.where(lanes == 127, reg_ref[...], value)
 
     for_parts(relay, 1, 0)
     for_parts(collect, 0, 1)
@@ -300,13 +319,13 @@
     for_parts(last_collect, 1)
 
     meta_copy.wait_send()
-    remote(turned_rx, turned_rx, pair_send.at[0], pair_recv.at[0], partner).wait_send()
+    remote(turned_rx, turned_rx, pair_send.at[0], pair_recv.at[4], partner).wait_send()
     for ph, place in enumerate((rx1, rx2, rx3)):
         remote(place, place, send_sem.at[ph], recv_sem.at[0], partner).wait_send()
 
 
-def gain_kernel(sums_ref, found_ref, reg_ref, gain_ref, leaf_ref, value_ref):
-    reg = reg_ref[0]
+def gain_kernel(sums_ref, found_ref, gain_ref, leaf_ref, value_ref):
+    reg = found_ref[0:1, 127:128]
     sums = sums_ref[...].reshape(192, 128)
     lane = lax.broadcasted_iota(jnp.int32, (128, 256), 0)
     col = lax.broadcasted_iota(jnp.int32, (128, 256), 1)
@@ -349,19 +368,24 @@
 def solution(mesh):
     row_spec = P(('trees', 'data'))
     vmem = pl.BlockSpec(memory_space=pltpu.VMEM)
-    smem = pl.BlockSpec(memory_space=pltpu.SMEM)
     hbm = pl.BlockSpec(memory_space=pl.ANY)
 
     def device_fn(bin_codes, gradient, hessian, valid_rows, split_feat, split_thr, cut_values, reg_lambda):
         sums, found = pl.pallas_call(
             hist_kernel,
-            out_shape=(jax.ShapeDtypeStruct((3, 2, 2, 2, 8, 128), F32), jax.ShapeDtypeStruct((1, 128), F32)),
-            in_specs=[hbm, vmem, vmem, smem, smem, smem, hbm],
+            out_shape=(pltpu.VMEM((3, 2, 2, 2, 8, 128), F32), pltpu.VMEM((1, 128), F32)),
+            in_specs=[hbm] * 8,
             out_specs=(vmem, vmem),
             scratch_shapes=[
+                pltpu.VMEM((1, ROWS), F32),
+                pltpu.VMEM((1, ROWS), F32),
+                pltpu.VMEM((1, 1), jnp.int32),
+                pltpu.SMEM((INNER,), jnp.int32),
+                pltpu.SMEM((INNER,), jnp.int32),
+                pltpu.VMEM((1, 1), F32),
                 pltpu.VMEM((LOADS, ROWS, SLAB), jnp.int32),
-                pltpu.VMEM((64, 2, 24, ROWS), F32),
-                pltpu.VMEM((64, 24, ROWS), F32),
+                pltpu.VMEM((4, 4, 4, 2, 24, ROWS), F32),
+                pltpu.VMEM((4, 4, 4, 24, ROWS), F32),
                 pltpu.VMEM((3, 4, 4, 4, 16, 2 * ROWS), BF16),
                 pltpu.VMEM((2, 8, ROWS), F32),
                 pltpu.VMEM((2 * ROWS, 256), BF16),
@@ -370,23 +394,23 @@
                 pltpu.VMEM((3, 2, 3, 2, 4, 8, 8, 128), F32),
                 pltpu.VMEM((3, 2, 3, 2, 8, 8, 128), F32),
                 pltpu.VMEM((3, 2, 3, 2, 2, 8, 128), F32),
-                pltpu.SemaphoreType.DMA((LOADS + 1,)),
+                pltpu.SemaphoreType.DMA((LOADS + 7,)),
                 pltpu.SemaphoreType.DMA((2,)),
-                pltpu.SemaphoreType.DMA((LOADS + 1,)),
+                pltpu.SemaphoreType.DMA((5,)),
                 pltpu.SemaphoreType.DMA((3,)),
                 pltpu.SemaphoreType.DMA((30,)),
             ],
             compiler_params=pltpu.CompilerParams(collective_id=0, has_side_effects=True, vmem_limit_bytes=60 * 1024 * 1024),
             name='hist',
-        )(bin_codes, gradient.reshape(1, ROWS), hessian.reshape(1, ROWS), valid_rows, split_feat, split_thr, cut_values.T)
+        )(bin_codes, gradient.reshape(1, ROWS), hessian.reshape(1, ROWS), valid_rows.reshape(1, 1), split_feat, split_thr, cut_values.T, reg_lambda.reshape(1, 1))
         gain, leaf, value = pl.pallas_call(
             gain_kernel,
             out_shape=(jax.ShapeDtypeStruct((BINS - 1, FEATS // 128, 63), F32), jax.ShapeDtypeStruct((1, LEAVES), F32), jax.ShapeDtypeStruct((1, INNER), F32)),
-            in_specs=[vmem, vmem, smem],
+            in_specs=[vmem, vmem],
             out_specs=(vmem, vmem, vmem),
             compiler_params=pltpu.CompilerParams(vmem_limit_bytes=4 * 1024 * 1024),
             name='gain',
-        )(sums, found, reg_lambda)
+        )(sums, found)
         return jnp.transpose(gain, (2, 1, 0)), leaf.reshape(LEAVES), value.reshape(INNER)
 
     return jax.shard_map(device_fn, mesh=mesh, in_specs=(P(('trees', 'data'), None), row_spec, row_spec, row_spec, P('trees'), P('trees'), P('trees', None), P('trees')), out_specs=(P(None, ('trees', 'data'), None), P('trees'), P('trees')), check_vma=False)

time: 53.4 us -> 49.5 us (0.927)
  Pallas kernels: 49.7 us -> 47.5 us
  local copies, waits for them, and re-layouts: 1.54 us -> 0 us
    pallas_call x1, Pallas kernels: 48.4 us -> 46.2 us  [device_fn(): pl.pallas_call(hist_kernel, out_shape=(pltpu.VMEM((3, 2, 2, 2, 8, 128), F...]
    unnamed x4 -> x0, local copies, waits for them, and re-layouts: 1.54 us -> none
where the time goes in v4:
time: 49.5 us; the launch traced here: 49.4 us
  Pallas kernels  47.5 us (96%)
  between operations  1.93 us (4%)
    pallas_call x1, Pallas kernels, device_fn(): pl.pallas_call(hist_kernel, out_shape=(pltpu.VMEM((3, 2, 2, 2, 8, 128), F...  46.2 us
    pallas_call x1, Pallas kernels, device_fn(): pl.pallas_call(gain_kernel, out_shape=(jax.ShapeDtypeStruct((BINS - 1, FE...  1.29 us

profile of v4, /device:TPU:0, one launch (start us, length us, event | category | flops | bytes accessed | tf_op | source)
XLA Modules:
  0.0 49.4 jit_solution(13647483213257208268)
XLA Ops:
  1.9 46.2 %hist.1 = (f32[3,2,2,2,8,128]{5,4,3,2,1,0:T(8,128)S(1)}, f32[1,128]{1,0:T(1,128)S(1)}) custom-call(s32[512,3072]{1,0:T(8,128)} %codes_hbm.1, f32[1,512]{1,0:T(1,128)} %bitcast.11, f32[1,512]{1,0:T(1,128)} %bitcast.12, s32[1,1]{1,0:T(1,128)} %bitcast.8.valid_hbm, s32[31]{0:T(128)} %feat_hbm.1, s32[31]{0:T(128)} %thr_hbm.1, f32[15,3072]{1,0:T(8,128)} %bitcast.10, ...), custom_call_target="tpu_custom_call" | custom-call | tf_op jit(solution)/shard_map/hist/pallas_call | solution.py:374
  48.1 1.3 %gain.1 = (f32[15,24,63]{2,1,0:T(8,128)}, f32[1,32]{1,0:T(1,128)}, f32[1,31]{1,0:T(1,128)}) custom-call(f32[3,2,2,2,8,128]{5,4,3,2,1,0:T(8,128)S(1)} %get-tuple-element.8.sums_ref, f32[1,128]{1,0:T(1,128)S(1)} %get-tuple-element.9.found_ref), custom_call_target="tpu_custom_call" | custom-call | tf_op jit(solution)/shard_map/gain/pallas_call | solution.py:406

commit v5 on v4

--- a/solution.py
+++ b/solution.py
@@ -264,11 +264,16 @@
         unit(zero, p, 0, ROWS, ROWS, True)
     for_parts(send_far, 0, 0)
 
+    def pick(b, *values):
+        return sum((b == k + 1).astype(jnp.int32) * v for k, v in enumerate(values))
+
     @pl.loop(1, 8)
     def _(b):
-        c, jj = b // 4, b % 4
-
-        @pl.when(c == 0)
+        item = (1 - core) * pick(b, 4, 6, 1, 2, 5, 7, 3) + core * pick(b, 1, 4, 2, 5, 7, 6, 3)
+        fresh = (1 - core) * pick(b, 0, 1, 1, 0, 0, 1, 0) + core * pick(b, 1, 0, 1, 0, 1, 0, 0)
+        c, jj = item // 4, item % 4
+
+        @pl.when(fresh == 1)
         def _():
             other_codes(jj)
 
@@ -289,15 +294,18 @@
             for p in range(3):
                 copy(0, c, p, 1, 0).start()
 
-        @pl.when(b == 3)
+        @pl.when((core == 0) & (b == 4))
         def _():
             for_parts(relay, 0, 0)
 
-        @pl.when(b == 6)
-        def _():
-            for_parts(collect, 0, 0)
-
-    for_parts(relay, 0, 1)
+        @pl.when((core == 0) & (b == 5))
+        def _():
+            for_parts(relay, 0, 1)
+
+    @pl.when(core == 1)
+    def _():
+        for_parts(relay, 0, 0)
+        for_parts(relay, 0, 1)
 
     pltpu.make_async_copy(cuts, cuts, load_sem.at[LOADS]).wait()
     lanes = lax.broadcasted_iota(jnp.int32, (1, 128), 1)
@@ -310,12 +318,13 @@
         value = jnp.where(lanes == j, one, value)
     value_ref[...] = jnp.where(lanes == 127, reg_ref[...], value)
 
+    for_parts(collect, 0, 0)
+    for_parts(collect, 0, 1)
     for_parts(relay, 1, 0)
-    for_parts(collect, 0, 1)
+    for_parts(relay, 1, 1)
     for_parts(collect, 1, 0)
-    for_parts(relay, 1, 1)
+    for_parts(collect, 1, 1)
     for_parts(last_collect, 0)
-    for_parts(collect, 1, 1)
     for_parts(last_collect, 1)
 
     meta_copy.wait_send()

time: 49.5 us -> 47 us (0.949)
  the two profiles are of different devices: /device:TPU:0 before, /device:TPU:1 now
where the time goes in v5:
time: 47 us; the launch traced here: 46.8 us
  Pallas kernels  44.9 us (96%)
  between operations  1.93 us (4%)
    pallas_call x1, Pallas kernels, device_fn(): pl.pallas_call(hist_kernel, out_shape=(pltpu.VMEM((3, 2, 2, 2, 8, 128), F...  43.6 us
    pallas_call x1, Pallas kernels, device_fn(): pl.pallas_call(gain_kernel, out_shape=(jax.ShapeDtypeStruct((BINS - 1, FE...  1.29 us

profile of v5, /device:TPU:1, one launch (start us, length us, event | category | flops | bytes accessed | tf_op | source)
XLA Modules:
  0.0 46.8 jit_solution(15523323844701750500)
XLA Ops:
  1.9 43.6 %hist.1 = (f32[3,2,2,2,8,128]{5,4,3,2,1,0:T(8,128)S(1)}, f32[1,128]{1,0:T(1,128)S(1)}) custom-call(s32[512,3072]{1,0:T(8,128)} %codes_hbm.1, f32[1,512]{1,0:T(1,128)} %bitcast.11, f32[1,512]{1,0:T(1,128)} %bitcast.12, s32[1,1]{1,0:T(1,128)} %bitcast.8.valid_hbm, s32[31]{0:T(128)} %feat_hbm.1, s32[31]{0:T(128)} %thr_hbm.1, f32[15,3072]{1,0:T(8,128)} %bitcast.10, ...), custom_call_target="tpu_custom_call" | custom-call | tf_op jit(solution)/shard_map/hist/pallas_call | solution.py:383
  45.5 1.3 %gain.1 = (f32[15,24,63]{2,1,0:T(8,128)}, f32[1,32]{1,0:T(1,128)}, f32[1,31]{1,0:T(1,128)}) custom-call(f32[3,2,2,2,8,128]{5,4,3,2,1,0:T(8,128)S(1)} %get-tuple-element.8.sums_ref, f32[1,128]{1,0:T(1,128)S(1)} %get-tuple-element.9.found_ref), custom_call_target="tpu_custom_call" | custom-call | tf_op jit(solution)/shard_map/gain/pallas_call | solution.py:415

commit v6 on v5

--- a/solution.py
+++ b/solution.py
@@ -15,6 +15,7 @@
 INNER = 31
 LOADS = 8
 SLAB = FEATS // LOADS
+GROUP = 128
 
 
 def pow4(dim):
@@ -123,7 +124,9 @@
 
     def goes_right(j):
         feat = feat_ref[j]
-        column = turned[feat // 768, feat // 192 % 4, feat // 48 % 4, feat // 24 % 2, pl.ds(feat % 24, 1), :]
+        owner = lax.div(feat, 24)
+        bits = [lax.shift_right_logical(owner, k) for k in (5, 3, 1, 0)]
+        column = turned[bits[0], bits[1] & 3, bits[2] & 3, bits[3] & 1, pl.ds(feat - 24 * owner, 1), :]
         return (column > thr_ref[j].astype(F32)).astype(jnp.int32)
 
     leaf = goes_right(0)
@@ -249,9 +252,11 @@
             both = both + hist[p, c, ja]
         hist[p, c, ja] = both
 
-    zero = jnp.int32(0)
-    for p in range(3):
-        unit(zero, p, 0, 0, ROWS, False)
+    @pl.loop(0, 1 + me // GROUP)
+    def _(z):
+        for p in range(3):
+            unit(z, p, z, 0, ROWS, False)
+
     other_codes(0)
     meta_copy.wait_recv()
     fill_weights(1)
@@ -260,8 +265,11 @@
         for p in range(3):
             task(*args, p)
 
-    for p in range(3):
-        unit(zero, p, 0, ROWS, ROWS, True)
+    @pl.loop(0, 1 + me // GROUP)
+    def _(z):
+        for p in range(3):
+            unit(z, p, z, ROWS, ROWS, True)
+
     for_parts(send_far, 0, 0)
 
     def pick(b, *values):
@@ -269,8 +277,8 @@
 
     @pl.loop(1, 8)
     def _(b):
-        item = (1 - core) * pick(b, 4, 6, 1, 2, 5, 7, 3) + core * pick(b, 1, 4, 2, 5, 7, 6, 3)
-        fresh = (1 - core) * pick(b, 0, 1, 1, 0, 0, 1, 0) + core * pick(b, 1, 0, 1, 0, 1, 0, 0)
+        item = (1 - core) * pick(b, 6, 4, 1, 2, 5, 7, 3) + core * pick(b, 4, 5, 6, 1, 2, 7, 3)
+        fresh = (1 - core) * pick(b, 1, 0, 1, 0, 0, 1, 0) + core * pick(b, 0, 1, 1, 0, 0, 1, 0)
         c, jj = item // 4, item % 4
 
         @pl.when(fresh == 1)
@@ -302,10 +310,9 @@
         def _():
             for_parts(relay, 0, 1)
 
-    @pl.when(core == 1)
-    def _():
-        for_parts(relay, 0, 0)
-        for_parts(relay, 0, 1)
+        @pl.when((core == 1) & (b == 6))
+        def _():
+            for_parts(relay, 0, 0)
 
     pltpu.make_async_copy(cuts, cuts, load_sem.at[LOADS]).wait()
     lanes = lax.broadcasted_iota(jnp.int32, (1, 128), 1)
@@ -317,6 +324,10 @@
         one = jnp.sum(jnp.where(lanes == feat % 128, one, 0.0), axis=1, keepdims=True)
         value = jnp.where(lanes == j, one, value)
     value_ref[...] = jnp.where(lanes == 127, reg_ref[...], value)
+
+    @pl.when(core == 1)
+    def _():
+        for_parts(relay, 0, 1)
 
     for_parts(collect, 0, 0)
     for_parts(collect, 0, 1)

time: 47 us -> 46.2 us (0.983)
  Pallas kernels: 44.9 us -> 44.1 us
    pallas_call x1, Pallas kernels: 43.6 us -> 42.8 us  [device_fn(): pl.pallas_call(hist_kernel, out_shape=(pltpu.VMEM((3, 2, 2, 2, 8, 128), F...]
where the time goes in v6:
time: 46.2 us; the launch traced here: 46.1 us
  Pallas kernels  44.1 us (95%)
  between operations  1.93 us (4%)
    pallas_call x1, Pallas kernels, device_fn(): pl.pallas_call(hist_kernel, out_shape=(pltpu.VMEM((3, 2, 2, 2, 8, 128), F...  42.8 us
    pallas_call x1, Pallas kernels, device_fn(): pl.pallas_call(gain_kernel, out_shape=(jax.ShapeDtypeStruct((BINS - 1, FE...  1.29 us

profile of v6, /device:TPU:1, one launch (start us, length us, event | category | flops | bytes accessed | tf_op | source)
XLA Modules:
  0.0 46.1 jit_solution(12982188783024878599)
XLA Ops:
  1.9 42.8 %hist.1 = (f32[3,2,2,2,8,128]{5,4,3,2,1,0:T(8,128)S(1)}, f32[1,128]{1,0:T(1,128)S(1)}) custom-call(s32[512,3072]{1,0:T(8,128)} %codes_hbm.1, f32[1,512]{1,0:T(1,128)} %bitcast.11, f32[1,512]{1,0:T(1,128)} %bitcast.12, s32[1,1]{1,0:T(1,128)} %bitcast.8.valid_hbm, s32[31]{0:T(128)} %feat_hbm.1, s32[31]{0:T(128)} %thr_hbm.1, f32[15,3072]{1,0:T(8,128)} %bitcast.10, ...), custom_call_target="tpu_custom_call" | custom-call | tf_op jit(solution)/shard_map/hist/pallas_call | solution.py:394
  44.8 1.3 %gain.1 = (f32[15,24,63]{2,1,0:T(8,128)}, f32[1,32]{1,0:T(1,128)}, f32[1,31]{1,0:T(1,128)}) custom-call(f32[3,2,2,2,8,128]{5,4,3,2,1,0:T(8,128)S(1)} %get-tuple-element.8.sums_ref, f32[1,128]{1,0:T(1,128)S(1)} %get-tuple-element.9.found_ref), custom_call_target="tpu_custom_call" | custom-call | tf_op jit(solution)/shard_map/gain/pallas_call | solution.py:426

commit v7 on v6

--- a/solution.py
+++ b/solution.py
@@ -55,7 +55,6 @@
     for dim in range(3):
         for step in (1, 2, 3):
             pl.semaphore_signal(barrier, inc=1, device_id=(0, neighbour(me, dim, step)), device_id_type=pl.DeviceIdType.MESH)
-    pl.semaphore_wait(barrier, 10)
 
     def ahead(jj):
         return (2 + 3 * jj + (jj // 2) * (7 - 2 * jj)) % 4
@@ -110,6 +109,7 @@
         fill_own(m - 1)
         turn(m)
 
+    pl.semaphore_wait(barrier, 10)
     for p in range(3):
         pair_copy(0, p).start()
 

time: 46.2 us -> 45.7 us (0.989)
  Pallas kernels: 44.1 us -> 43.6 us
    pallas_call x1, Pallas kernels: 42.8 us -> 42.3 us  [device_fn(): pl.pallas_call(hist_kernel, out_shape=(pltpu.VMEM((3, 2, 2, 2, 8, 128), F...]
where the time goes in v7:
time: 45.7 us; the launch traced here: 45.6 us
  Pallas kernels  43.6 us (95%)
  between operations  1.93 us (4%)
    pallas_call x1, Pallas kernels, device_fn(): pl.pallas_call(hist_kernel, out_shape=(pltpu.VMEM((3, 2, 2, 2, 8, 128), F...  42.3 us
    pallas_call x1, Pallas kernels, device_fn(): pl.pallas_call(gain_kernel, out_shape=(jax.ShapeDtypeStruct((BINS - 1, FE...  1.29 us

profile of v7, /device:TPU:1, one launch (start us, length us, event | category | flops | bytes accessed | tf_op | source)
XLA Modules:
  0.0 45.6 jit_solution(7598987431133530256)
XLA Ops:
  1.9 42.3 %hist.1 = (f32[3,2,2,2,8,128]{5,4,3,2,1,0:T(8,128)S(1)}, f32[1,128]{1,0:T(1,128)S(1)}) custom-call(s32[512,3072]{1,0:T(8,128)} %codes_hbm.1, f32[1,512]{1,0:T(1,128)} %bitcast.11, f32[1,512]{1,0:T(1,128)} %bitcast.12, s32[1,1]{1,0:T(1,128)} %bitcast.8.valid_hbm, s32[31]{0:T(128)} %feat_hbm.1, s32[31]{0:T(128)} %thr_hbm.1, f32[15,3072]{1,0:T(8,128)} %bitcast.10, ...), custom_call_target="tpu_custom_call" | custom-call | tf_op jit(solution)/shard_map/hist/pallas_call | solution.py:394
  44.3 1.3 %gain.1 = (f32[15,24,63]{2,1,0:T(8,128)}, f32[1,32]{1,0:T(1,128)}, f32[1,31]{1,0:T(1,128)}) custom-call(f32[3,2,2,2,8,128]{5,4,3,2,1,0:T(8,128)S(1)} %get-tuple-element.8.sums_ref, f32[1,128]{1,0:T(1,128)S(1)} %get-tuple-element.9.found_ref), custom_call_target="tpu_custom_call" | custom-call | tf_op jit(solution)/shard_map/gain/pallas_call | solution.py:426

commit v8 on v7

--- a/solution.py
+++ b/solution.py
@@ -33,7 +33,8 @@
 
 def hist_kernel(codes_hbm, grad_hbm, hess_hbm, valid_hbm, feat_hbm, thr_hbm, cut_hbm, reg_hbm, out_ref, value_ref,
                 grad_ref, hess_ref, valid_ref, feat_ref, thr_ref, reg_ref, raw, turned, turned_rx, codes2, meta, weights, cuts, hist, rx1, rx2, rx3,
-                load_sem, pair_send, pair_recv, send_sem, recv_sem):
+                load_sem, small_sem, pair_recv, recv_sem):
+    sent = load_sem
     me = lax.axis_index('data')
     core = me % 2
     partner = me + 1 - 2 * core
@@ -46,7 +47,7 @@
 
     for m in range(LOADS):
         load(m).start()
-    small = [pltpu.make_async_copy(src, dst, load_sem.at[LOADS + 1 + k]) for k, (src, dst) in enumerate(
+    small = [pltpu.make_async_copy(src, dst, small_sem.at[k]) for k, (src, dst) in enumerate(
         ((grad_hbm, grad_ref), (hess_hbm, hess_ref), (valid_hbm, valid_ref), (feat_hbm, feat_ref), (thr_hbm, thr_ref), (reg_hbm, reg_ref)))]
     for one in small:
         one.start()
@@ -69,9 +70,9 @@
             src, dst = turned.at[:, ja, :, other, rows], turned_rx.at[:, ja, :, rows]
         else:
             src, dst = turned.at[ja, :, :, other, rows], turned_rx.at[ja, :, :, rows]
-        return remote(src, dst, pair_send.at[0], pair_recv.at[jj], partner)
-
-    meta_copy = remote(meta.at[0], meta.at[1], pair_send.at[1], pair_recv.at[4], partner)
+        return remote(src, dst, sent.at[3], pair_recv.at[jj], partner)
+
+    meta_copy = remote(meta.at[0], meta.at[1], sent.at[4], pair_recv.at[4], partner)
 
     def put_code(p, ja, jb, jc, lane0, v):
         codes2[p, ja, jb, jc, :, pl.ds(lane0, ROWS)] = jnp.concatenate([v, v - 1.0], axis=0).astype(BF16)
@@ -93,7 +94,7 @@
                     put_code(p, ja, jb, jc, ROWS, turned_rx[z, y, x, pl.ds(8 * p, 8), :])
 
     def other_codes(jj):
-        remote(turned_rx.at[0], turned_rx.at[0], pair_send.at[0], pair_recv.at[jj], partner).wait_recv()
+        remote(turned_rx.at[0], turned_rx.at[0], sent.at[3], pair_recv.at[jj], partner).wait_recv()
         fill_other(jj)
 
     def turn(m):
@@ -115,7 +116,7 @@
 
     @pl.loop(0, FEATS // 128)
     def _(k):
-        pltpu.make_async_copy(cut_hbm.at[:, pl.ds(k * 128, 128)], cuts.at[k], load_sem.at[LOADS]).start()
+        pltpu.make_async_copy(cut_hbm.at[:, pl.ds(k * 128, 128)], cuts.at[k], load_sem.at[5]).start()
 
     fill_own(LOADS - 1)
 
@@ -177,13 +178,13 @@
         at = coord(me, dim)
         step = 1 if (kind == 1) == (half == 1) else -1
         j = (at + 2) % 4 if kind == 0 else (at + step + 4) % 4
-        s = ((ph * 2 + c) * 3 + p) * 2 + (0 if kind == 0 else 1)
-        return remote(block(ph, c, p, half, j), landings[ph].at[p, c, kind, half], send_sem.at[ph], recv_sem.at[s], neighbour(me, dim, step))
+        s = (ph * 2 + c) * 2 + (0 if kind == 0 else 1)
+        return remote(block(ph, c, p, half, j), landings[ph].at[p, c, kind, half], sent.at[ph], recv_sem.at[s], neighbour(me, dim, step))
 
     def wait_landed(ph, c, p, kind, count):
-        s = ((ph * 2 + c) * 3 + p) * 2 + (0 if kind == 0 else 1)
-        place = landings[ph].at[p, c, pl.ds(kind, count)]
-        remote(place, place, send_sem.at[ph], recv_sem.at[s], partner).wait_recv()
+        if p == 0:
+            place = landings[ph].at[:, c, pl.ds(kind, count)]
+            remote(place, place, sent.at[ph], recv_sem.at[(ph * 2 + c) * 2 + (0 if kind == 0 else 1)], partner).wait_recv()
 
     def send_far(ph, c, p):
         copy(ph, c, p, 0, 0).start()
@@ -221,10 +222,11 @@
     def last_copy(c, p, step):
         dim = (p + 2) % 3
         j = (coord(me, dim) + step) % 4
-        return remote(last_block(c, p, j), rx3.at[p, c, step - 1], send_sem.at[2], recv_sem.at[24 + 3 * c + p], neighbour(me, dim, step))
+        return remote(last_block(c, p, j), rx3.at[p, c, step - 1], sent.at[2], recv_sem.at[8 + c], neighbour(me, dim, step))
 
     def last_collect(c, p):
-        remote(rx3.at[p, c], rx3.at[p, c], send_sem.at[2], recv_sem.at[24 + 3 * c + p], partner).wait_recv()
+        if p == 0:
+            remote(rx3.at[:, c], rx3.at[:, c], sent.at[2], recv_sem.at[8 + c], partner).wait_recv()
         out_ref[p, c] = last_block(c, p, coord(me, (p + 2) % 3))[...] + rx3[p, c, 0] + rx3[p, c, 1] + rx3[p, c, 2]
 
     first_half = lax.broadcasted_iota(jnp.int32, (64, 8, 128), 2) < 64
@@ -314,7 +316,7 @@
         def _():
             for_parts(relay, 0, 0)
 
-    pltpu.make_async_copy(cuts, cuts, load_sem.at[LOADS]).wait()
+    pltpu.make_async_copy(cuts, cuts, load_sem.at[5]).wait()
     lanes = lax.broadcasted_iota(jnp.int32, (1, 128), 1)
     steps = lax.broadcasted_iota(jnp.int32, (BINS - 1, 128), 0)
     value = jnp.zeros((1, 128), F32)
@@ -339,9 +341,9 @@
     for_parts(last_collect, 1)
 
     meta_copy.wait_send()
-    remote(turned_rx, turned_rx, pair_send.at[0], pair_recv.at[4], partner).wait_send()
+    remote(turned_rx, turned_rx, sent.at[3], pair_recv.at[4], partner).wait_send()
     for ph, place in enumerate((rx1, rx2, rx3)):
-        remote(place, place, send_sem.at[ph], recv_sem.at[0], partner).wait_send()
+        remote(place, place, sent.at[ph], recv_sem.at[0], partner).wait_send()
 
 
 def gain_kernel(sums_ref, found_ref, gain_ref, leaf_ref, value_ref):
@@ -414,11 +416,10 @@
                 pltpu.VMEM((3, 2, 3, 2, 4, 8, 8, 128), F32),
                 pltpu.VMEM((3, 2, 3, 2, 8, 8, 128), F32),
                 pltpu.VMEM((3, 2, 3, 2, 2, 8, 128), F32),
-                pltpu.SemaphoreType.DMA((LOADS + 7,)),
-                pltpu.SemaphoreType.DMA((2,)),
+                pltpu.SemaphoreType.DMA((LOADS,)),
+                pltpu.SemaphoreType.DMA((6,)),
                 pltpu.SemaphoreType.DMA((5,)),
-                pltpu.SemaphoreType.DMA((3,)),
-                pltpu.SemaphoreType.DMA((30,)),
+                pltpu.SemaphoreType.DMA((10,)),
             ],
             compiler_params=pltpu.CompilerParams(collective_id=0, has_side_effects=True, vmem_limit_bytes=60 * 1024 * 1024),
             name='hist',

time: 45.7 us -> 44.8 us (0.980)
  Pallas kernels: 43.6 us -> 42.8 us
    pallas_call x1, Pallas kernels: 42.3 us -> 41.5 us  [device_fn(): pl.pallas_call(hist_kernel, out_shape=(pltpu.VMEM((3, 2, 2, 2, 8, 128), F...]
where the time goes in v8:
time: 44.8 us; the launch traced here: 44.7 us
  Pallas kernels  42.8 us (96%)
  between operations  1.93 us (4%)
    pallas_call x1, Pallas kernels, device_fn(): pl.pallas_call(hist_kernel, out_shape=(pltpu.VMEM((3, 2, 2, 2, 8, 128), F...  41.5 us
    pallas_call x1, Pallas kernels, device_fn(): pl.pallas_call(gain_kernel, out_shape=(jax.ShapeDtypeStruct((BINS - 1, FE...  1.29 us

profile of v8, /device:TPU:1, one launch (start us, length us, event | category | flops | bytes accessed | tf_op | source)
XLA Modules:
  0.0 44.7 jit_solution(14067274897365201509)
XLA Ops:
  1.9 41.5 %hist.1 = (f32[3,2,2,2,8,128]{5,4,3,2,1,0:T(8,128)S(1)}, f32[1,128]{1,0:T(1,128)S(1)}) custom-call(s32[512,3072]{1,0:T(8,128)} %codes_hbm.1, f32[1,512]{1,0:T(1,128)} %bitcast.11, f32[1,512]{1,0:T(1,128)} %bitcast.12, s32[1,1]{1,0:T(1,128)} %bitcast.8.valid_hbm, s32[31]{0:T(128)} %feat_hbm.1, s32[31]{0:T(128)} %thr_hbm.1, f32[15,3072]{1,0:T(8,128)} %bitcast.10, ...), custom_call_target="tpu_custom_call" | custom-call | tf_op jit(solution)/shard_map/hist/pallas_call | solution.py:396
  43.4 1.3 %gain.1 = (f32[15,24,63]{2,1,0:T(8,128)}, f32[1,32]{1,0:T(1,128)}, f32[1,31]{1,0:T(1,128)}) custom-call(f32[3,2,2,2,8,128]{5,4,3,2,1,0:T(8,128)S(1)} %get-tuple-element.8.sums_ref, f32[1,128]{1,0:T(1,128)S(1)} %get-tuple-element.9.found_ref), custom_call_target="tpu_custom_call" | custom-call | tf_op jit(solution)/shard_map/gain/pallas_call | solution.py:427

commit v9 on v8

--- a/solution.py
+++ b/solution.py
@@ -42,8 +42,10 @@
     def remote(src, dst, s_sem, r_sem, device):
         return pltpu.make_async_remote_copy(src_ref=src, dst_ref=dst, send_sem=s_sem, recv_sem=r_sem, device_id=(0, device), device_id_type=pl.DeviceIdType.MESH)
 
+    first = 2 * ((coord(me, 2) + 2) % 4)
+
     def load(m):
-        return pltpu.make_async_copy(codes_hbm.at[:, pl.ds(m * SLAB, SLAB)], raw.at[m], load_sem.at[m])
+        return pltpu.make_async_copy(codes_hbm.at[:, pl.ds((m + first) % LOADS * SLAB, SLAB)], raw.at[m], load_sem.at[m])
 
     for m in range(LOADS):
         load(m).start()
@@ -70,7 +72,7 @@
             src, dst = turned.at[:, ja, :, other, rows], turned_rx.at[:, ja, :, rows]
         else:
             src, dst = turned.at[ja, :, :, other, rows], turned_rx.at[ja, :, :, rows]
-        return remote(src, dst, sent.at[3], pair_recv.at[jj], partner)
+        return remote(src, dst, small_sem.at[6], pair_recv.at[jj], partner)
 
     meta_copy = remote(meta.at[0], meta.at[1], sent.at[4], pair_recv.at[4], partner)
 
@@ -78,6 +80,7 @@
         codes2[p, ja, jb, jc, :, pl.ds(lane0, ROWS)] = jnp.concatenate([v, v - 1.0], axis=0).astype(BF16)
 
     def fill_own(m):
+        m = (m + first) % LOADS
         z = m // 2
         for k in range(8):
             y, x = m % 2 * 2 + k // 4, k % 4
@@ -94,12 +97,13 @@
                     put_code(p, ja, jb, jc, ROWS, turned_rx[z, y, x, pl.ds(8 * p, 8), :])
 
     def other_codes(jj):
-        remote(turned_rx.at[0], turned_rx.at[0], sent.at[3], pair_recv.at[jj], partner).wait_recv()
+        remote(turned_rx.at[0], turned_rx.at[0], small_sem.at[6], pair_recv.at[jj], partner).wait_recv()
         fill_other(jj)
 
     def turn(m):
         block = raw[m].astype(F32).astype(BF16)
-        turned[m // 2, pl.ds(m % 2 * 2, 2)] = block.T.astype(F32).reshape(2, 4, 2, 24, ROWS)
+        at = (m + first) % LOADS
+        turned[at // 2, pl.ds(at % 2 * 2, 2)] = block.T.astype(F32).reshape(2, 4, 2, 24, ROWS)
 
     load(0).wait()
     turn(0)
@@ -110,8 +114,12 @@
         fill_own(m - 1)
         turn(m)
 
-    pl.semaphore_wait(barrier, 10)
-    for p in range(3):
+        @pl.when(m == 3)
+        def _():
+            pl.semaphore_wait(barrier, 10)
+            pair_copy(0, 2).start()
+
+    for p in range(2):
         pair_copy(0, p).start()
 
     @pl.loop(0, FEATS // 128)
@@ -341,7 +349,7 @@
     for_parts(last_collect, 1)
 
     meta_copy.wait_send()
-    remote(turned_rx, turned_rx, sent.at[3], pair_recv.at[4], partner).wait_send()
+    remote(turned_rx, turned_rx, small_sem.at[6], pair_recv.at[4], partner).wait_send()
     for ph, place in enumerate((rx1, rx2, rx3)):
         remote(place, place, sent.at[ph], recv_sem.at[0], partner).wait_send()
 
@@ -417,7 +425,7 @@
                 pltpu.VMEM((3, 2, 3, 2, 8, 8, 128), F32),
                 pltpu.VMEM((3, 2, 3, 2, 2, 8, 128), F32),
                 pltpu.SemaphoreType.DMA((LOADS,)),
-                pltpu.SemaphoreType.DMA((6,)),
+                pltpu.SemaphoreType.DMA((7,)),
                 pltpu.SemaphoreType.DMA((5,)),
                 pltpu.SemaphoreType.DMA((10,)),
             ],

time: 44.8 us -> 44.4 us (level)
  no operation moved by 1% of the time
where the time goes in v9:
time: 44.4 us; the launch traced here: 44.3 us
  Pallas kernels  42.4 us (95%)
  between operations  1.93 us (4%)
    pallas_call x1, Pallas kernels, device_fn(): pl.pallas_call(hist_kernel, out_shape=(pltpu.VMEM((3, 2, 2, 2, 8, 128), F...  41.1 us
    pallas_call x1, Pallas kernels, device_fn(): pl.pallas_call(gain_kernel, out_shape=(jax.ShapeDtypeStruct((BINS - 1, FE...  1.29 us

profile of v9, /device:TPU:1, one launch (start us, length us, event | category | flops | bytes accessed | tf_op | source)
XLA Modules:
  0.0 44.3 jit_solution(17784844098902714900)
XLA Ops:
  1.9 41.1 %hist.1 = (f32[3,2,2,2,8,128]{5,4,3,2,1,0:T(8,128)S(1)}, f32[1,128]{1,0:T(1,128)S(1)}) custom-call(s32[512,3072]{1,0:T(8,128)} %codes_hbm.1, f32[1,512]{1,0:T(1,128)} %bitcast.11, f32[1,512]{1,0:T(1,128)} %bitcast.12, s32[1,1]{1,0:T(1,128)} %bitcast.8.valid_hbm, s32[31]{0:T(128)} %feat_hbm.1, s32[31]{0:T(128)} %thr_hbm.1, f32[15,3072]{1,0:T(8,128)} %bitcast.10, ...), custom_call_target="tpu_custom_call" | custom-call | tf_op jit(solution)/shard_map/hist/pallas_call | solution.py:404
  43.0 1.3 %gain.1 = (f32[15,24,63]{2,1,0:T(8,128)}, f32[1,32]{1,0:T(1,128)}, f32[1,31]{1,0:T(1,128)}) custom-call(f32[3,2,2,2,8,128]{5,4,3,2,1,0:T(8,128)S(1)} %get-tuple-element.8.sums_ref, f32[1,128]{1,0:T(1,128)S(1)} %get-tuple-element.9.found_ref), custom_call_target="tpu_custom_call" | custom-call | tf_op jit(solution)/shard_map/gain/pallas_call | solution.py:435

commit v10 on v9

--- a/solution.py
+++ b/solution.py
@@ -114,7 +114,7 @@
         fill_own(m - 1)
         turn(m)
 
-        @pl.when(m == 3)
+        @pl.when(m == 2)
         def _():
             pl.semaphore_wait(barrier, 10)
             pair_copy(0, 2).start()
@@ -370,7 +370,7 @@
     rest = sums - hi.astype(F32)
     mid = rest.astype(BF16)
     low = (rest - mid.astype(F32)).astype(BF16)
-    nodes = jnp.dot(low, pick, preferred_element_type=F32) + jnp.dot(mid, pick, preferred_element_type=F32) + jnp.dot(hi, pick, preferred_element_type=F32)
+    nodes = jnp.dot(jnp.concatenate([low, mid, hi], axis=1), jnp.concatenate([pick] * 3, axis=0), preferred_element_type=F32)
     grad = nodes[:, :128].reshape(3, 8, 8, 128)
     hess = nodes[:, 128:].reshape(3, 8, 8, 128)
     upper = lax.broadcasted_iota(jnp.int32, (8, 128), 1) >= 64

time: 44.4 us -> 44.4 us (level)
  no operation moved by 1% of the time
where the time goes in v10:
time: 44.4 us; the launch traced here: 44.3 us
  Pallas kernels  42.4 us (95%)
  between operations  1.93 us (4%)
    pallas_call x1, Pallas kernels, device_fn(): pl.pallas_call(hist_kernel, out_shape=(pltpu.VMEM((3, 2, 2, 2, 8, 128), F...  41.1 us
    pallas_call x1, Pallas kernels, device_fn(): pl.pallas_call(gain_kernel, out_shape=(jax.ShapeDtypeStruct((BINS - 1, FE...  1.27 us

profile of v10, /device:TPU:1, one launch (start us, length us, event | category | flops | bytes accessed | tf_op | source)
XLA Modules:
  0.0 44.3 jit_solution(5783055924750644506)
XLA Ops:
  1.9 41.1 %hist.1 = (f32[3,2,2,2,8,128]{5,4,3,2,1,0:T(8,128)S(1)}, f32[1,128]{1,0:T(1,128)S(1)}) custom-call(s32[512,3072]{1,0:T(8,128)} %codes_hbm.1, f32[1,512]{1,0:T(1,128)} %bitcast.11, f32[1,512]{1,0:T(1,128)} %bitcast.12, s32[1,1]{1,0:T(1,128)} %bitcast.8.valid_hbm, s32[31]{0:T(128)} %feat_hbm.1, s32[31]{0:T(128)} %thr_hbm.1, f32[15,3072]{1,0:T(8,128)} %bitcast.10, ...), custom_call_target="tpu_custom_call" | custom-call | tf_op jit(solution)/shard_map/hist/pallas_call | solution.py:404
  43.0 1.3 %gain.1 = (f32[15,24,63]{2,1,0:T(8,128)}, f32[1,32]{1,0:T(1,128)}, f32[1,31]{1,0:T(1,128)}) custom-call(f32[3,2,2,2,8,128]{5,4,3,2,1,0:T(8,128)S(1)} %get-tuple-element.8.sums_ref, f32[1,128]{1,0:T(1,128)S(1)} %get-tuple-element.9.found_ref), custom_call_target="tpu_custom_call" | custom-call | tf_op jit(solution)/shard_map/gain/pallas_call | solution.py:435
